TPU v7x, 256 devices: a whole 4x4x8 slice. The times are simulated.
256 devices in a mesh: row: 32 (over z_lo, y, core), col: 8 (over x, z_hi).
Axes of the slice: x: 4, y: 4, z: 8 (z_hi: 2, z_lo: 4; z = z_hi * 4 + z_lo), core: 2. Of those that a mesh axis runs over, the one named last changes fastest.
Arguments:
- pair_rep: bfloat16 [2048, 2048, 128], P('row', 'col'), may hold values from -6 to 6
- bias_weight: bfloat16 [128, 12], replicated, may hold values from -0.5 to 0.5
- head_weight: float32 [12], replicated, may hold values from -1 to 1
- queries: float32 [192, 2048], P(None, 'row'), may hold values from -48 to 48, as said below
- key_vectors: float32 [192, 2048], P(None, 'col'), may hold values from -48 to 48, as said below
- values: float32 [192, 2048], P(None, 'col'), may hold values from -6 to 6
- query_points: float32 [3, 48, 2048], P(None, None, 'row'), may hold values from -6 to 6
- key_points: float32 [3, 48, 2048], P(None, None, 'col'), may hold values from -6 to 6
- value_points: float32 [3, 96, 2048], P(None, None, 'col'), may hold values from -6 to 6
- rotations: float32 [3, 3, 2048], replicated, may hold values from -1 to 1, as said below
- translations: float32 [3, 2048], replicated, may hold values from -12 to 12
- residue_count: int32 [1], replicated, may hold values from 1024 to 2048
- grad_output: float32 [192, 2048], P(None, 'row'), may hold values from -6 to 6
- grad_points: float32 [3, 96, 2048], P(None, None, 'row'), may hold values from -6 to 6
- grad_pair: bfloat16 [2048, 12, 128], P('row'), may hold values from -2 to 2
Outputs:
- pair_grad: bfloat16 [2048, 2048, 128], P('row', 'col')
- query_grad: float32 [192, 2048], P(None, ('row', 'col'))
- query_point_grad: float32 [3, 48, 2048], P(None, None, ('row', 'col'))
- query_frame_grad: float32 [3, 4, 2048], P(None, None, ('row', 'col'))
- key_grad: float32 [192, 2048], P(None, ('col', 'row'))
- value_grad: float32 [192, 2048], P(None, ('col', 'row'))
- key_point_grad: float32 [3, 48, 2048], P(None, None, ('col', 'row'))
- value_point_grad: float32 [3, 96, 2048], P(None, None, ('col', 'row'))
- key_frame_grad: float32 [3, 4, 2048], P(None, None, ('col', 'row'))
- bias_weight_grad: float32 [128, 12], replicated
- head_weight_grad: float32 [12], replicated
Inputs may be any that keep to these rules, and one draw needn't show every extreme that they name: `queries`: entries of order one, except a few residues whose vectors are much larger. `key_vectors`: entries of order one, except a few residues whose vectors are much larger. `rotations`: each residue's 3 x 3 matrix is a rotation: orthonormal with determinant one.
All inputs are finite; a program needn't handle non-finite values.
Results may differ from a plain program's by a relative error of at most 0.0049.
Values sent between devices are 32-bit elements; how exact they have to be, the bound alone decides.
A program may use at most 128 MiB of HBM per device.

v0:
```python
import functools
import math

import jax
import jax.numpy as jnp
from jax import lax
from jax.sharding import Mesh
from jax.sharding import PartitionSpec as P

ROW = ("row_0", "row_1", "row_2")
COL = ("col_0", "col_1")
ROW_COL = ("row_0", "row_1", "row_2", "col_0", "col_1")
COL_ROW = ("col_0", "col_1", "row_0", "row_1", "row_2")


HIGHEST = lax.Precision.HIGHEST


def from_everyone(shard, axis):
    count = lax.axis_size(axis)
    return lax.all_to_all(
        jnp.broadcast_to(shard[None], (count, *shard.shape)), axis, 0, 0, tiled=True
    )


def over_copies(shard, axis):
    return from_everyone(shard, axis).max(axis=0)


def over_copies_2(shard, axis):
    return from_everyone(shard, axis).sum(axis=0)


def packed_total(arrays, axis):
    ends = [0]
    for a in arrays:
        ends.append(ends[-1] + a.size)
    total = over_copies_2(jnp.concatenate([a.ravel() for a in arrays]), axis)
    return tuple((total[b:e].reshape(a.shape) for a, b, e in zip(arrays, ends, ends[1:])))


def split_up(shard, dim, count):
    before, after = (shard.shape[:dim], shard.shape[dim + 1 :])
    return jnp.moveaxis(shard.reshape(*before, count, -1, *after), dim, 0)


def sum_at_owner(shard, axis, dim):
    count = lax.axis_size(axis)
    parts = lax.all_to_all(split_up(shard, dim, count), axis, 0, 0, tiled=True)
    return jnp.sum(parts, axis=0)


def sum_packed(arrays, axis, dims):
    count = lax.axis_size(axis)
    parts = [split_up(a, dim, count) for a, dim in zip(arrays, dims)]
    lines = jnp.concatenate([b.reshape(count, -1) for b in parts], axis=1)
    rows = max(16, -(-lines.shape[1] // 1024) * 8)
    lines = jnp.pad(lines, ((0, 0), (0, rows * 128 - lines.shape[1]))).reshape(-1, 128)
    flat, at, finished = (lax.psum_scatter(lines, axis, tiled=True).reshape(-1), 0, [])
    for b in parts:
        part = b[0]
        finished.append(flat[at : at + part.size].reshape(part.shape))
        at += part.size
    return tuple(finished)


def by_axis(shard, axes):
    return functools.reduce(lax.psum, axes, shard)


def globalize(rotation, offset, local):
    return jnp.einsum("xym,ykm->xkm", rotation, local, precision=HIGHEST) + offset[:, None, :]


def rotate_back(rotation, vector):
    return jnp.einsum("xym,xkm->ykm", rotation, vector, precision=HIGHEST)


def frame_terms(grad_global, local):
    rotation_part = jnp.einsum("xkm,ykm->xym", grad_global, local, precision=HIGHEST)
    return jnp.concatenate([rotation_part, jnp.sum(grad_global, axis=1)[:, None, :]], axis=1)


def output_frame_terms(point_out, offset, cotan_local, grad_rotated):
    rotation_part = jnp.einsum(
        "xkm,ykm->xym", point_out - offset[:, None, :], cotan_local, precision=HIGHEST
    )
    return jnp.concatenate([rotation_part, -jnp.sum(grad_rotated, axis=1)[:, None, :]], axis=1)


def per_device(
    pair_rep,
    bias_weight,
    head_weight,
    queries,
    key_vectors,
    values,
    query_points,
    key_points,
    value_points,
    rotations,
    translations,
    residue_count,
    grad_output,
    grad_points,
    grad_pair,
):
    heads = bias_weight.shape[1]
    width = queries.shape[0] // heads
    qpoints = query_points.shape[1] // heads
    vpoints = value_points.shape[1] // heads
    rows_here = queries.shape[1]
    cols_here = key_vectors.shape[1]
    logit_scale = math.sqrt(1.0 / 3.0)
    point_scale = math.sqrt(2.0 / (9.0 * qpoints))
    inner_scale = 1.0 / math.sqrt(width)
    distance_coef = 0.5 * logit_scale * point_scale * jax.nn.softplus(head_weight)
    row_start = lax.axis_index(ROW) * rows_here
    col_start = lax.axis_index(COL) * cols_here
    rot_rows = lax.dynamic_slice_in_dim(rotations, row_start, rows_here, 2)
    shift_rows = lax.dynamic_slice_in_dim(translations, row_start, rows_here, 1)
    rot_cols = lax.dynamic_slice_in_dim(rotations, col_start, cols_here, 2)
    shift_cols = lax.dynamic_slice_in_dim(translations, col_start, cols_here, 1)
    query_global = globalize(rot_rows, shift_rows, query_points).reshape(
        3, heads, qpoints, rows_here
    )
    key_global = globalize(rot_cols, shift_cols, key_points).reshape(3, heads, qpoints, cols_here)
    value_global = globalize(rot_cols, shift_cols, value_points).reshape(
        3, heads, vpoints, cols_here
    )
    grad_flat = jnp.einsum("xym,ykm->xkm", rot_rows, grad_points, precision=HIGHEST)
    grad_heads = grad_flat.reshape(3, heads, vpoints, rows_here)
    query_heads = queries.reshape(heads, width, rows_here)
    out_heads = grad_output.reshape(heads, width, rows_here)
    key_heads = key_vectors.reshape(heads, width, cols_here)
    value_heads = values.reshape(heads, width, cols_here)
    valid = col_start + lax.iota(jnp.int32, cols_here) < residue_count[0]
    inner = jnp.einsum("hci,hcj->hij", query_heads, key_heads, precision=HIGHEST)
    cross = jnp.einsum("xhpi,xhpj->hij", query_global, key_global, precision=HIGHEST)
    distance = (
        jnp.sum(query_global**2, axis=(0, 2))[:, :, None]
        + jnp.sum(key_global**2, axis=(0, 2))[:, None, :]
        - 2.0 * cross
    )
    bias = jnp.einsum("ijc,ch->hij", pair_rep, bias_weight, preferred_element_type=jnp.float32)
    logits = logit_scale * (inner_scale * inner + bias) - distance_coef[:, None, None] * distance
    logits = jnp.where(valid[None, None, :], logits, jnp.float32(-1000000000.0))
    product = (
        jnp.einsum("hci,hcj->hij", out_heads, value_heads, precision=HIGHEST)
        + jnp.einsum("xhvi,xhvj->hij", grad_heads, value_global, precision=HIGHEST)
        + jnp.einsum("ijc,ihc->hij", pair_rep, grad_pair, preferred_element_type=jnp.float32)
    )
    row_peak = over_copies(jnp.max(logits, axis=2), COL)
    exponent = jnp.exp(logits - row_peak[:, :, None])
    row_total, row_upper, row_points = packed_total(
        (
            jnp.sum(exponent, axis=2),
            jnp.sum(exponent * product, axis=2),
            jnp.einsum("hij,xhvj->xhvi", exponent, value_global, precision=HIGHEST),
        ),
        COL,
    )
    attention = exponent / row_total[:, :, None]
    delta = row_upper / row_total
    point_out = (row_points / row_total[None, :, None, :]).reshape(3, heads * vpoints, rows_here)
    logit_grad = attention * (product - delta[:, :, None])
    grad_rounded = logit_grad.astype(jnp.bfloat16)
    attn_rounded = attention.astype(jnp.bfloat16)
    pair_grad = (
        logit_scale
        * jnp.einsum("hij,ch->ijc", grad_rounded, bias_weight, preferred_element_type=jnp.float32)
        + jnp.einsum("hij,ihc->ijc", attn_rounded, grad_pair, preferred_element_type=jnp.float32)
    ).astype(jnp.bfloat16)
    weight_part = logit_scale * jnp.einsum(
        "ijc,hij->ch", pair_rep, grad_rounded, preferred_element_type=jnp.float32
    )
    distance_part = jnp.sum(logit_grad * distance, axis=(1, 2))
    query_part = (
        logit_scale
        * inner_scale
        * jnp.einsum("hij,hcj->hci", logit_grad, key_heads, precision=HIGHEST)
    )
    row_sum = jnp.sum(logit_grad, axis=2)
    qpoint_part = (
        -2.0
        * distance_coef[None, :, None, None]
        * (
            query_global * row_sum[None, :, None, :]
            - jnp.einsum("hij,xhpj->xhpi", logit_grad, key_global, precision=HIGHEST)
        )
    )
    query_grad, qpoint_sum = (
        sum_at_owner(query_part.reshape(heads * width, rows_here), COL, 1),
        sum_at_owner(qpoint_part.reshape(3, heads * qpoints, rows_here), COL, 2),
    )
    share = rows_here // lax.axis_size(COL)
    share_start = lax.axis_index(COL) * share
    own_start = row_start + share_start
    rot_own = lax.dynamic_slice_in_dim(rotations, own_start, share, 2)
    shift_own = lax.dynamic_slice_in_dim(translations, own_start, share, 1)
    local_own = lax.dynamic_slice_in_dim(query_points, share_start, share, 2)
    cotan_own = lax.dynamic_slice_in_dim(grad_points, share_start, share, 2)
    out_own = lax.dynamic_slice_in_dim(point_out, share_start, share, 2)
    rotated_own = lax.dynamic_slice_in_dim(grad_flat, share_start, share, 2)
    query_point_grad = rotate_back(rot_own, qpoint_sum)
    query_frame_grad = frame_terms(qpoint_sum, local_own) + output_frame_terms(
        out_own, shift_own, cotan_own, rotated_own
    )
    key_part = (
        logit_scale
        * inner_scale
        * jnp.einsum("hij,hci->hcj", logit_grad, query_heads, precision=HIGHEST)
    )
    value_part = jnp.einsum("hij,hci->hcj", attention, out_heads, precision=HIGHEST)
    col_sum = jnp.sum(logit_grad, axis=1)
    kpoint_part = (
        2.0
        * distance_coef[None, :, None, None]
        * (
            jnp.einsum("hij,xhpi->xhpj", logit_grad, query_global, precision=HIGHEST)
            - key_global * col_sum[None, :, None, :]
        )
    ).reshape(3, heads * qpoints, cols_here)
    vpoint_part = jnp.einsum("hij,xhvi->xhvj", attention, grad_heads, precision=HIGHEST).reshape(
        3, heads * vpoints, cols_here
    )
    key_flat = key_part.reshape(heads * width, cols_here)
    value_flat = value_part.reshape(heads * width, cols_here)
    key_grad, value_grad, kpoint_sum, vpoint_sum = sum_packed(
        (key_flat, value_flat, kpoint_part, vpoint_part), ROW, (1, 1, 2, 2)
    )
    kshare = cols_here // lax.axis_size(ROW)
    kshare_start = lax.axis_index(ROW) * kshare
    rot_keys = lax.dynamic_slice_in_dim(rotations, col_start + kshare_start, kshare, 2)
    klocal_own = lax.dynamic_slice_in_dim(key_points, kshare_start, kshare, 2)
    vlocal_own = lax.dynamic_slice_in_dim(value_points, kshare_start, kshare, 2)
    key_point_grad = rotate_back(rot_keys, kpoint_sum)
    value_point_grad = rotate_back(rot_keys, vpoint_sum)
    key_frame_grad = frame_terms(kpoint_sum, klocal_own) + frame_terms(vpoint_sum, vlocal_own)
    weight_total, distance_total = (by_axis(weight_part, ROW_COL), by_axis(distance_part, ROW_COL))
    head_weight_grad = (
        distance_total * (-0.5 * logit_scale * point_scale) * jax.nn.sigmoid(head_weight)
    )
    return (
        pair_grad,
        query_grad,
        query_point_grad,
        query_frame_grad,
        key_grad,
        value_grad,
        key_point_grad,
        value_point_grad,
        key_frame_grad,
        weight_total,
        head_weight_grad,
    )


def solution(mesh):
    finer = Mesh(mesh.devices.reshape(4, 4, 2, 4, 2), ("row_0", "row_1", "row_2", "col_0", "col_1"))
    in_specs = (
        P(ROW, COL, None),
        P(),
        P(),
        P(None, ROW),
        P(None, COL),
        P(None, COL),
        P(None, None, ROW),
        P(None, None, COL),
        P(None, None, COL),
        P(),
        P(),
        P(),
        P(None, ROW),
        P(None, None, ROW),
        P(ROW, None, None),
    )
    out_specs = (
        P(ROW, COL, None),
        P(None, ROW_COL),
        P(None, None, ROW_COL),
        P(None, None, ROW_COL),
        P(None, COL_ROW),
        P(None, COL_ROW),
        P(None, None, COL_ROW),
        P(None, None, COL_ROW),
        P(None, None, COL_ROW),
        P(),
        P(),
    )
    return jax.shard_map(
        per_device, mesh=finer, in_specs=in_specs, out_specs=out_specs, check_vma=False
    )
```

profile of v0, /device:TPU:1, one launch (start us, length us, event | category | flops | bytes accessed | tf_op | source)
XLA Modules:
  0.0 415.0 jit_solution(17823779164322360788)
XLA Ops:
  10.8 1.2 broadcast_multiply_fusion
  12.6 0.9 copy.420
  13.9 1.0 copy.423
  16.0 1.1 copy.427
  17.1 2.0 multiply_reduce_fusion.2
  19.6 3.5 fusion.44
  23.1 0.9 fusion.2
  24.0 1.4 fusion.59
  26.2 11.5 %all-to-all-start = ((f32[8,1,768]{2,1,0:T(1,128)}), f32[8,1,768]{2,1,0:T(1,128)S(1)}, u32[]{:S(2)}, u32[]{:S(2)}) async-start(f32[8,1,768]{2,1,0:T(1,128)} %reshape.192), calls=%async_computation | async-start | bytes 49152 | tf_op jit(solution)/shard_map/all_to_all | solution.py:21
  38.7 2.6 fusion.7
  41.3 1.2 copy.438
  42.5 3.4 fusion.31
  45.9 0.8 convolution_bitcast_fusion
  46.8 0.9 copy.433
  49.1 0.9 convolution_bitcast_fusion.7
  50.1 3.1 fusion.27
  53.4 1.2 broadcast_in_dim.25
  54.5 9.0 %all-to-all-start.1 = ((f32[8,1,19968]{2,1,0:T(1,128)}), f32[8,1,19968]{2,1,0:T(1,128)S(1)}, u32[]{:S(2)}, u32[]{:S(2)}) async-start(f32[8,1,19968]{2,1,0:T(1,128)} %broadcast_in_dim.25), calls=%async_computation.1 | async-start | bytes 1277952 | tf_op jit(solution)/shard_map/all_to_all | solution.py:21
  65.5 0.8 constant_dynamic-slice_fusion
  68.7 10.0 %all-to-all-done.1 = f32[8,1,19968]{2,1,0:T(1,128)S(1)} async-done(((f32[8,1,19968]{2,1,0:T(1,128)}), f32[8,1,19968]{2,1,0:T(1,128)S(1)}, u32[]{:S(2)}, u32[]{:S(2)}) %all-to-all-start.1) | async-done | bytes 639008 | tf_op jit(solution)/shard_map/all_to_all | solution.py:21
  79.3 2.6 multiply_reduce_fusion
  82.5 1.4 fusion.13
  85.4 1.4 fusion.17
  86.8 4.5 %fusion.23 = f32[64,256,128]{2,1,0:T(8,128)} fusion(bf16[12,64,256]{2,1,0:T(8,128)(2,1)S(1)} %convert_element_type.11, bf16[128,12]{0,1:T(8,128)(2,1)S(1)} %copy-done.31), kind=kOutput, calls=%fused_computation.54 | convolution fusion | flops 50331648 | bytes 8784896 | tf_op jit(solution)/shard_map/hij,ch->ijc/dot_general | solution.py:171
  95.7 4.0 all-to-all-start.3
  100.0 1.3 copy.466
  102.3 0.9 copy.476
  103.3 1.3 copy.464
  105.6 0.9 copy.475
  106.5 1.3 reshape_reshape.22
  108.7 4.7 %reshape_reshape.23 = f32[3,96,32,8]{3,2,1,0:T(8,128)} reshape(f32[3,12,8,256]{3,2,1,0:T(8,128)} %copy.473) | data formatting | bytes 589824 | tf_op jit(solution)/shard_map/reshape;reshape | solution.py:44
  113.4 3.1 copy.474
  117.0 1.1 reshape.179
  118.1 13.9 %all-reduce.4 = (f32[128,12]{0,1:T(8,128)S(1)}, f32[12]{0:T(128)S(1)}) all-reduce(f32[128,12]{0,1:T(8,128)S(1)} %copy-done.29, f32[12]{0:T(128)S(1)} %copy-done.33), channel_id=1, replica_groups=mesh['row_0'=4,'row_1'=4,'row_2'=2,'col_0'=4,'col_1'=2] {'row_0'}, use_global_device_ids=true, to_apply=%region_18.19 | all-reduce | flops 1548 | bytes 12384 | tf_op jit(solution)/shard_map/psum | solution.py:68
  132.0 9.0 %all-reduce.3 = (f32[128,12]{0,1:T(8,128)S(1)}, f32[12]{0:T(128)S(1)}) all-reduce(f32[128,12]{0,1:T(8,128)S(1)} %get-tuple-element.99, f32[12]{0:T(128)S(1)} %get-tuple-element.100), channel_id=1, replica_groups=mesh['row_0'=4,'row_1'=4,'row_2'=2,'col_0'=4,'col_1'=2] {'row_1'}, use_global_device_ids=true, to_apply=%region_19.20 | all-reduce | flops 1548 | bytes 12384 | tf_op jit(solution)/shard_map/psum | solution.py:68
  141.0 7.9 %all-reduce.6 = (f32[128,12]{0,1:T(8,128)S(1)}, f32[12]{0:T(128)S(1)}) all-reduce(f32[128,12]{0,1:T(8,128)S(1)} %get-tuple-element.97, f32[12]{0:T(128)S(1)} %get-tuple-element.98), channel_id=1, replica_groups=mesh['row_0'=4,'row_1'=4,'row_2'=2,'col_0'=4,'col_1'=2] {'row_2'}, use_global_device_ids=true, to_apply=%region_20.21 | all-reduce | flops 1548 | bytes 12384 | tf_op jit(solution)/shard_map/psum | solution.py:68
  148.9 9.6 %all-reduce.2 = (f32[128,12]{0,1:T(8,128)S(1)}, f32[12]{0:T(128)S(1)}) all-reduce(f32[128,12]{0,1:T(8,128)S(1)} %get-tuple-element.103, f32[12]{0:T(128)S(1)} %get-tuple-element.104), channel_id=1, replica_groups=mesh['row_0'=4,'row_1'=4,'row_2'=2,'col_0'=4,'col_1'=2] {'col_0'}, use_global_device_ids=true, to_apply=%region_21.22 | all-reduce | flops 1548 | bytes 12384 | tf_op jit(solution)/shard_map/psum | solution.py:68
  158.5 8.4 %all-reduce.5 = (f32[128,12]{0,1:T(8,128)}, f32[12]{0:T(128)S(1)}) all-reduce(f32[128,12]{0,1:T(8,128)S(1)} %get-tuple-element.95, f32[12]{0:T(128)S(1)} %get-tuple-element.96), channel_id=1, replica_groups=mesh['row_0'=4,'row_1'=4,'row_2'=2,'col_0'=4,'col_1'=2] {'col_1'}, use_global_device_ids=true, to_apply=%region_22.23 | all-reduce | flops 1548 | bytes 12384 | tf_op jit(solution)/shard_map/psum | solution.py:68
  166.9 7.4 %add_convert_fusion = bf16[64,256,128]{2,1,0:T(8,128)(2,1)} fusion(f32[64,256,128]{2,1,0:T(8,128)} %fusion.23, bf16[12,64,256]{2,1,0:T(8,128)(2,1)S(1)} %get-tuple-element.110, bf16[64,12,128]{2,0,1:T(8,128)(2,1)S(1)} %copy-done.4), kind=kOutput, calls=%fused_computation | convolution fusion | flops 56623104 | bytes 13172736 | tf_op jit(solution)/shard_map/hij,ihc->ijc/dot_general | solution.py:172
  174.4 0.9 convolution_bitcast_fusion.14
  176.2 0.8 reshape_reshape.18
  177.0 6.7 %all-to-all-start.2 = ((f32[8,192,8]{1,2,0:T(8,128)}), f32[8,192,8]{1,2,0:T(8,128)S(1)}, u32[]{:S(2)}, u32[]{:S(2)}) async-start(f32[8,192,8]{1,2,0:T(8,128)} %bitcast.21), calls=%async_computation.2 | async-start | bytes 131072 | tf_op jit(solution)/shard_map/all_to_all | solution.py:49
  183.8 1.5 reduce.8
  185.7 0.9 convolution_bitcast_fusion.15
  187.3 5.6 %all-to-all-done.2 = f32[8,192,8]{1,2,0:T(8,128)S(1)} async-done(((f32[8,192,8]{1,2,0:T(8,128)}), f32[8,192,8]{1,2,0:T(8,128)S(1)}, u32[]{:S(2)}, u32[]{:S(2)}) %all-to-all-start.2) | async-done | bytes 49184 | tf_op jit(solution)/shard_map/all_to_all | solution.py:49
  193.5 206.1 %all-reduce.9.cloned.1.call-done = f32[1792,128]{1,0:T(8,128)} async-done(((f32[1792,128]{1,0:T(8,128)}), f32[1792,128]{1,0:T(8,128)}) %all-reduce.9.cloned.1.call-update) | async-done | bytes 917520
  401.5 0.9 convolution_bitcast_fusion.11
  402.6 0.9 convolution_bitcast_fusion.10
  (184 shorter events, 32.0 us)
Async XLA Ops:
  7.2 16.8 %copy-start = (f32[192,256]{1,0:T(8,128)S(1)}, f32[192,256]{1,0:T(8,128)}, u32[]{:S(2)}) copy-start(f32[192,256]{1,0:T(8,128)} %param.19) | copy-start | bytes 589828
  7.2 12.4 %copy-start.30 = (bf16[128,12]{0,1:T(8,128)(2,1)S(1)}, bf16[128,12]{0,1:T(8,128)(2,1)}, u32[]{:S(2)}) copy-start(bf16[128,12]{0,1:T(8,128)(2,1)} %param.16) | copy-start | bytes 9220
  13.6 10.5 %copy-start.7 = (f32[192,64]{1,0:T(8,128)}, f32[192,64]{1,0:T(8,128)S(1)}, u32[]{:S(2)}) copy-start(f32[192,64]{1,0:T(8,128)S(1)} %copy.420) | copy-start | bytes 147460
  13.9 9.2 %copy-start.25 = (f32[3,256]{0,1:T(8,128)}, f32[3,256]{0,1:T(8,128)S(1)}, u32[]{:S(2)}) copy-start(f32[3,256]{0,1:T(8,128)S(1)} %copy.428) | copy-start | bytes 9220
  14.9 4.3 %copy-start.22 = (f32[3,48,64]{1,0,2:T(4,128)}, f32[3,48,64]{1,0,2:T(4,128)S(1)}, u32[]{:S(2)}) copy-start(f32[3,48,64]{1,0,2:T(4,128)S(1)} %copy.423) | copy-start | bytes 110596
  15.7 7.4 %copy-start.11 = (f32[3,48,64]{2,1,0:T(8,128)}, f32[3,48,64]{2,1,0:T(8,128)S(1)}, u32[]{:S(2)}) copy-start(f32[3,48,64]{2,1,0:T(8,128)S(1)} %copy.430) | copy-start | bytes 110596
  17.1 2.2 copy-start.15
  19.6 4.4 %copy-start.5 = (f32[3,12,4,256]{3,2,1,0:T(4,128)}, f32[3,12,4,256]{3,2,1,0:T(4,128)S(1)}, u32[]{:S(2)}) copy-start(f32[3,12,4,256]{3,2,1,0:T(4,128)S(1)} %reshape.165) | copy-start | bytes 442372
  19.6 18.1 %copy-start.17 = (f32[3,96,64]{1,2,0:T(8,128)S(1)}, f32[3,96,64]{1,2,0:T(8,128)}, u32[]{:S(2)}) copy-start(f32[3,96,64]{1,2,0:T(8,128)} %param.28) | copy-start | bytes 221188
  19.6 18.8 %copy-start.21 = (f32[3,96,256]{2,1,0:T(8,128)S(1)}, f32[3,96,256]{2,1,0:T(8,128)}, u32[]{:S(2)}) copy-start(f32[3,96,256]{2,1,0:T(8,128)} %param.23) | copy-start | bytes 884740
  23.1 15.6 %copy-start.26 = (f32[3,256]{0,1:T(8,128)S(1)}, f32[3,256]{0,1:T(8,128)}, u32[]{:S(2)}) copy-start(f32[3,256]{0,1:T(8,128)} %copy-done.25) | copy-start | bytes 9220
  23.1 19.4 %copy-start.3 = (bf16[64,12,128]{2,0,1:T(8,128)(2,1)S(1)}, bf16[64,12,128]{2,0,1:T(8,128)(2,1)}, u32[]{:S(2)}) copy-start(bf16[64,12,128]{2,0,1:T(8,128)(2,1)} %param.29) | copy-start | bytes 589828
  24.0 1.5 copy-start.2
  26.2 21.5 %all-to-all-start = ((f32[8,1,768]{2,1,0:T(1,128)}), f32[8,1,768]{2,1,0:T(1,128)S(1)}, u32[]{:S(2)}, u32[]{:S(2)}) async-start(f32[8,1,768]{2,1,0:T(1,128)} %reshape.192), calls=%async_computation | async-start | bytes 49152 | tf_op jit(solution)/shard_map/all_to_all | solution.py:21
  38.4 7.5 %copy-start.13 = (f32[3,96,64]{2,1,0:T(8,128)}, f32[3,96,64]{2,1,0:T(8,128)S(1)}, u32[]{:S(2)}) copy-start(f32[3,96,64]{2,1,0:T(8,128)S(1)} %copy.435) | copy-start | bytes 221188
  38.6 3.9 copy-start.16
  46.8 17.5 %copy-start.37 = (u32[256]{0:T(256)S(1)}, u32[256]{0:T(256)}, u32[]{:S(2)}) copy-start(u32[256]{0:T(256)} %constant.67) | copy-start | bytes 3076
  47.7 31.4 %copy-start.19 = (f32[192,64]{1,0:T(8,128)}, f32[192,64]{1,0:T(8,128)S(1)}, u32[]{:S(2)}) copy-start(f32[192,64]{1,0:T(8,128)S(1)} %copy.433) | copy-start | bytes 147460
  49.1 30.0 %copy-start.23 = (f32[12,64]{1,0:T(8,128)}, f32[12,64]{1,0:T(8,128)S(1)}, u32[]{:S(2)}) copy-start(f32[12,64]{1,0:T(8,128)S(1)} %reduce_max.19) | copy-start | bytes 9220
  53.2 28.7 %copy-start.8 = (f32[192,64]{1,0:T(8,128)S(1)}, f32[192,64]{1,0:T(8,128)}, u32[]{:S(2)}) copy-start(f32[192,64]{1,0:T(8,128)} %copy-done.7) | copy-start | bytes 147460
  54.5 24.1 %all-to-all-start.1 = ((f32[8,1,19968]{2,1,0:T(1,128)}), f32[8,1,19968]{2,1,0:T(1,128)S(1)}, u32[]{:S(2)}, u32[]{:S(2)}) async-start(f32[8,1,19968]{2,1,0:T(1,128)} %broadcast_in_dim.25), calls=%async_computation.1 | async-start | bytes 1277952 | tf_op jit(solution)/shard_map/all_to_all | solution.py:21
  79.1 4.8 %copy-start.20 = (f32[192,64]{1,0:T(8,128)S(1)}, f32[192,64]{1,0:T(8,128)}, u32[]{:S(2)}) copy-start(f32[192,64]{1,0:T(8,128)} %copy-done.19) | copy-start | bytes 147460
  79.1 4.8 %copy-start.24 = (f32[12,64]{1,0:T(8,128)S(1)}, f32[12,64]{1,0:T(8,128)}, u32[]{:S(2)}) copy-start(f32[12,64]{1,0:T(8,128)} %copy-done.23) | copy-start | bytes 9220
  79.3 5.4 %copy-start.14 = (f32[3,96,64]{2,1,0:T(8,128)S(1)}, f32[3,96,64]{2,1,0:T(8,128)}, u32[]{:S(2)}) copy-start(f32[3,96,64]{2,1,0:T(8,128)} %copy-done.13) | copy-start | bytes 221188
  82.4 3.0 copy-start.1
  84.7 2.1 copy-start.31
  86.8 4.6 %copy-start.6 = (f32[3,12,4,256]{3,2,1,0:T(4,128)S(1)}, f32[3,12,4,256]{3,2,1,0:T(4,128)}, u32[]{:S(2)}) copy-start(f32[3,12,4,256]{3,2,1,0:T(4,128)} %copy-done.5) | copy-start | bytes 442372
  86.8 4.6 %copy-start.12 = (f32[3,48,64]{2,1,0:T(8,128)S(1)}, f32[3,48,64]{2,1,0:T(8,128)}, u32[]{:S(2)}) copy-start(f32[3,48,64]{2,1,0:T(8,128)} %copy-done.11) | copy-start | bytes 110596
  86.8 4.6 %copy-start.35 = (f32[12]{0:T(128)S(1)}, f32[12]{0:T(128)}, u32[]{:S(2)}) copy-start(f32[12]{0:T(128)} %get-tuple-element.105) | copy-start | bytes 148
  86.8 5.2 %copy-start.34 = (f32[12]{0:T(128)S(1)}, f32[12]{0:T(128)}, u32[]{:S(2)}) copy-start(f32[12]{0:T(128)} %get-tuple-element.115) | copy-start | bytes 148
  95.7 81.3 %all-to-all-start.3 = ((f32[8,1,1152]{2,1,0:T(1,128)}), f32[8,1,1152]{2,1,0:T(1,128)}, u32[]{:S(2)}, u32[]{:S(2)}) async-start(f32[8,1,1152]{2,1,0:T(1,128)} %reshape.194), calls=%async_computation.3 | async-start | bytes 73728 | tf_op jit(solution)/shard_map/all_to_all | solution.py:49
  99.7 299.9 %all-reduce.9.cloned.1.call-start = ((), (), s32[]{:S(2)}) async-start(), calls=%async_computation.4 | async-start | bytes 1835008
  113.4 3.5 copy-start.9
  113.4 3.5 copy-start.10
  116.5 1.6 copy-start.29
  116.5 1.5 copy-start.33
  116.5 50.4 %copy-start.4 = (bf16[64,12,128]{2,0,1:T(8,128)(2,1)S(1)}, bf16[64,12,128]{2,0,1:T(8,128)(2,1)}, u32[]{:S(2)}) copy-start(bf16[64,12,128]{2,0,1:T(8,128)(2,1)} %param.29) | copy-start | bytes 589828
  166.9 7.5 %copy-start.27 = (f32[3,96,8]{1,0,2:T(4,128)S(1)}, f32[3,96,8]{1,0,2:T(4,128)}, u32[]{:S(2)}) copy-start(f32[3,96,8]{1,0,2:T(4,128)} %copy.460) | copy-start | bytes 27652
  166.9 8.4 %copy-start.36 = (f32[12]{0:T(128)S(1)}, f32[12]{0:T(128)}, u32[]{:S(2)}) copy-start(f32[12]{0:T(128)} %param.17) | copy-start | bytes 148
  166.9 9.0 %copy-start.18 = (f32[12,16,64]{2,1,0:T(8,128)S(1)}, f32[12,16,64]{2,1,0:T(8,128)}, u32[]{:S(2)}) copy-start(f32[12,16,64]{2,1,0:T(8,128)} %fusion.13) | copy-start | bytes 147460
  166.9 18.5 %copy-start.28 = (f32[3,3,8]{0,1,2:T(4,128)S(1)}, f32[3,3,8]{0,1,2:T(4,128)}, u32[]{:S(2)}) copy-start(f32[3,3,8]{0,1,2:T(4,128)} %copy.508) | copy-start | bytes 868
  166.9 240.6 %copy-start.32 = (f32[3,1,8]{2,1,0:T(1,128)S(1)}, f32[3,1,8]{2,1,0:T(1,128)}, u32[]{:S(2)}) copy-start(f32[3,1,8]{2,1,0:T(1,128)} %copy.463) | copy-start | bytes 292
  177.0 15.8 %all-to-all-start.2 = ((f32[8,192,8]{1,2,0:T(8,128)}), f32[8,192,8]{1,2,0:T(8,128)S(1)}, u32[]{:S(2)}, u32[]{:S(2)}) async-start(f32[8,192,8]{1,2,0:T(8,128)} %bitcast.21), calls=%async_computation.2 | async-start | bytes 131072 | tf_op jit(solution)/shard_map/all_to_all | solution.py:49
Sparse Core Ops, SparseCore 0:
  118.2 281.3 all-reduce.8
where the time goes:
time: 418 us; the launch traced here: 415 us
  waiting for transfers between devices  222 us (53%)
  blocking collectives  48.8 us (12%)
  local copies, waits for them, and re-layouts  45.3 us (11%)
  matrix products  42.1 us (10%)
  starting transfers between devices  31.5 us (8%)
  between operations  16.3 us (4%)
  other arithmetic  9.25 us (2%)
    unnamed x2, waiting for transfers between devices  206 us
    psum x5, blocking collectives, by_axis(): return functools.reduce(lax.psum, axes, shard)  48.8 us
    all_to_all x2, starting transfers between devices, from_everyone(): lax.all_to_all(jnp.broadcast_to(shard[None], (count, *shard.shape)), axis...  20.5 us
    unnamed x96, local copies, waits for them, and re-layouts  11.8 us
    all_to_all x2, starting transfers between devices, sum_at_owner(): parts = lax.all_to_all(split_up(shard, dim, count), axis, 0, 0, tiled=True)  10.7 us
    all_to_all x2, waiting for transfers between devices, from_everyone(): lax.all_to_all(jnp.broadcast_to(shard[None], (count, *shard.shape)), axis...  9.97 us
    another operation x6, local copies, waits for them, and re-layouts, split_up(): return jnp.moveaxis(shard.reshape(*before, count, -1, *after), dim, 0)  8.47 us
  transfers between devices with their start and end apart: 5, of which 3 were waited for; matrix products, arithmetic and copies ran while one was open for 11% of the time, Pallas kernels for 0%

commit v1 on v0

v1 whole, which is shorter than its diff:
```python
import functools
import math

import jax
import jax.numpy as jnp
from jax import lax
from jax.experimental import pallas as pl
from jax.experimental.pallas import tpu as pltpu
from jax.sharding import Mesh
from jax.sharding import PartitionSpec as P

ROW = ("row_0", "row_1", "row_2")
COL = ("col_0", "col_1")
ROW_COL = ROW + COL
COL_ROW = COL + ROW

H, C, PQ, PV, CZ = 12, 16, 4, 8, 128
KF, QF = 896, 768
VAL0, KP0, VP0 = 192, 384, 528
LOGIT = math.sqrt(1.0 / 3.0)
POINT = math.sqrt(2.0 / (9.0 * PQ))
INNER = 1.0 / math.sqrt(C)

F32, BF = jnp.float32, jnp.bfloat16
HIGHEST = lax.Precision.HIGHEST
MESH = pl.DeviceIdType.MESH


def dot(a, b, ca, cb, precision=None):
    return lax.dot_general(
        a, b, (((ca,), (cb,)), ((), ())), precision=precision, preferred_element_type=F32
    )


def split(a):
    hi = a.astype(BF)
    return hi, (a - hi.astype(F32)).astype(BF)


def dot3(a, b, ca, cb):
    (ah, al), (bh, bl) = a, b
    return dot(ah, bh, ca, cb) + dot(ah, bl, ca, cb) + dot(al, bh, ca, cb)


def iota(shape, dim):
    return lax.broadcasted_iota(jnp.int32, shape, dim)


def softplus(x):
    return jnp.maximum(x, 0.0) + jnp.log1p(jnp.exp(-jnp.abs(x)))


def tile_kernel(
    sizes,
    pair_hbm,
    wt_ref,
    hw_ref,
    q_ref,
    k_ref,
    v_ref,
    qp_ref,
    kp_ref,
    vp_ref,
    rot_ref,
    trans_ref,
    count_ref,
    go_ref,
    gp_ref,
    gpair_ref,
    pg_hbm,
    key_out,
    query_out,
    small_out,
    pair_v,
    pg_v,
    s_ref,
    e_ref,
    p_ref,
    d_ref,
    q32,
    k32,
    g48,
    v48,
    vec,
    vec_t,
    stat_own,
    stat_in,
    feat,
    kt,
    k1,
    p1,
    k2,
    p2,
    k3,
    qfeat,
    qt,
    qin,
    w_own,
    w_in,
    w_mid,
    w_in2,
    pair_sem,
    pg_sem,
    stat_send,
    stat_recv,
    k1_send,
    k1_recv,
    k2_send,
    k2_recv,
    k3_send,
    k3_recv,
    q_send,
    q_recv,
    w_send,
    w_recv,
    w2_send,
    w2_recv,
):
    n0, n1, n2, m0, m1 = sizes
    cols_n = m0 * m1
    rows = q_ref.shape[0]
    cols = k_ref.shape[1]
    i0, i1, i2 = (lax.axis_index(a) for a in ROW)
    j0, j1 = (lax.axis_index(a) for a in COL)
    r = (i0 * n1 + i1) * n2 + i2
    c = j0 * m1 + j1

    def col_peer(d):
        p = lax.rem(c + d, cols_n)
        return {"col_0": p // m1, "col_1": lax.rem(p, m1)}

    g1 = cols_n * n2
    g2 = n0 * n1

    def one_peer(d):
        p = lax.rem(c * n2 + i2 + d, g1)
        pc = p // n2
        return {"col_0": pc // m1, "col_1": lax.rem(pc, m1), "row_2": lax.rem(p, n2)}

    def two_peer(d):
        p = lax.rem(i0 * n1 + i1 + d, g2)
        return {"row_0": p // n1, "row_1": lax.rem(p, n1)}

    core_peer = {"row_2": lax.rem(i2 + 1, n2)}

    barrier = pltpu.get_barrier_semaphore()
    for d in range(1, g1):
        pl.semaphore_signal(barrier, inc=1, device_id=one_peer(d), device_id_type=MESH)
    for d in range(1, g2):
        pl.semaphore_signal(barrier, inc=1, device_id=two_peer(d), device_id_type=MESH)

    parts = pair_sem.shape[0]
    step = rows // parts
    loads = [
        pltpu.make_async_copy(
            pair_hbm.at[pl.ds(b * step, step)], pair_v.at[pl.ds(b * step, step)], pair_sem.at[b]
        )
        for b in range(parts)
    ]
    for load in loads:
        load.start()

    col_start = pl.multiple_of(c * cols, 128)
    row_start = r * rows
    row_base = pl.multiple_of((row_start // 128) * 128, 128)
    row_half = lax.rem(row_start, 128)

    def row_window(w):
        return jnp.where(row_half == 0, w[:, :rows], w[:, 128 - rows :])

    def row_rot(x, y):
        return row_window(rot_ref[x, pl.ds(y, 1), pl.ds(row_base, 128)])

    def col_rot(x, y):
        return rot_ref[x, pl.ds(y, 1), pl.ds(col_start, cols)]

    coef = 0.5 * LOGIT * POINT * softplus(hw_ref[...])

    zero_q = jnp.zeros((2, rows), F32)
    zero_k = jnp.zeros((2, cols), F32)
    q_t = q_ref[...].T * (LOGIT * INNER)
    k_all = k_ref[...]
    rr = [[row_rot(x, y) for y in range(3)] for x in range(3)]
    cr = [[col_rot(x, y) for y in range(3)] for x in range(3)]
    for x in range(3):
        t_row = row_window(trans_ref[pl.ds(x, 1), pl.ds(row_base, 128)])
        t_col = trans_ref[pl.ds(x, 1), pl.ds(col_start, cols)]
        qg = sum(rr[x][y] * qp_ref[y] for y in range(3)) + t_row
        kg = sum(cr[x][y] * kp_ref[y] for y in range(3)) + t_col
        vg = sum(cr[x][y] * vp_ref[y] for y in range(3)) + t_col
        for h in range(H):
            q32[32 * h + 16 + 4 * x : 32 * h + 20 + 4 * x, :] = qg[4 * h : 4 * h + 4]
            k32[32 * h + 16 + 4 * x : 32 * h + 20 + 4 * x, :] = kg[4 * h : 4 * h + 4]
            v48[48 * h + 16 + 8 * x : 48 * h + 24 + 8 * x, :] = vg[8 * h : 8 * h + 8]
    gp_t = [gp_ref[y].T for y in range(3)]
    for x in range(3):
        gg = sum(rr[x][y] * gp_t[y] for y in range(3))
        for h in range(H):
            g48[48 * h + 16 + 8 * x : 48 * h + 24 + 8 * x, :] = gg[8 * h : 8 * h + 8]
    go_t = go_ref[...].T
    for h in range(H):
        q32[32 * h : 32 * h + 16, :] = q_t[16 * h : 16 * h + 16]
        k32[32 * h : 32 * h + 16, :] = k_all[16 * h : 16 * h + 16]
        g48[48 * h : 48 * h + 16, :] = go_t[16 * h : 16 * h + 16]
        v48[48 * h : 48 * h + 16, :] = v_ref[16 * h : 16 * h + 16, :]
        g48[48 * h + 40 : 48 * h + 48, :] = jnp.zeros((8, rows), F32)
        v48[48 * h + 40 : 48 * h + 48, :] = jnp.zeros((8, cols), F32)
        qh = q32[32 * h + 16 : 32 * h + 28, :]
        kh = k32[32 * h + 16 : 32 * h + 28, :]
        q32[32 * h + 28 : 32 * h + 32, :] = jnp.concatenate(
            [jnp.sum(qh * qh, axis=0, keepdims=True), jnp.ones((1, rows), F32), zero_q], axis=0
        )
        k32[32 * h + 28 : 32 * h + 32, :] = jnp.concatenate(
            [jnp.ones((1, cols), F32), jnp.sum(kh * kh, axis=0, keepdims=True), zero_k], axis=0
        )

    def pair_row(at):
        return jnp.concatenate(
            [s_ref[a, pl.ds(at, rows, stride=32), :] for a in range(cols // 128)], axis=1
        )

    def put_pair_row(at, value):
        for a in range(cols // 128):
            s_ref[a, pl.ds(at, rows, stride=32), :] = value[:, 128 * a : 128 * a + 128]

    def pair_block(at, count):
        return jnp.concatenate(
            [s_ref[a, at : at + count, :] for a in range(cols // 128)], axis=1
        )

    w16 = jnp.concatenate([wt_ref[...].astype(F32), jnp.zeros((4, CZ), F32)], axis=0)
    w16b = w16.astype(BF)

    def stack(i):
        gpad = jnp.concatenate(
            [gpair_ref[:, i, :].astype(F32), jnp.zeros((4, CZ), F32)], axis=0
        ).astype(BF)
        return gpad

    for b in range(parts):
        loads[b].wait()
        for ii in range(step):
            i = b * step + ii
            both = jnp.concatenate([w16b, stack(i)], axis=0)
            proj = dot(both, pair_v[i], 1, 1)
            for a in range(cols // 128):
                s_ref[a, 32 * i : 32 * i + 32, :] = proj[:, 128 * a : 128 * a + 128]

    point_row = iota((16, 1), 0) < 12
    valid = col_start + iota((1, cols), 1) < count_ref[0]
    lane = iota((rows, 128), 1)
    for h in range(H):
        qa = q32[32 * h : 32 * h + 16, :]
        qb = q32[32 * h + 16 : 32 * h + 32, :]
        kb = k32[32 * h + 16 : 32 * h + 32, :]
        inner = dot(qa, k32[32 * h : 32 * h + 16, :], 0, 0, HIGHEST)
        dist = dot(qb, jnp.where(point_row, -2.0 * kb, kb), 0, 0, HIGHEST)
        prod = dot3(
            split(g48[48 * h : 48 * h + 48, :]), split(v48[48 * h : 48 * h + 48, :]), 0, 0
        )
        prod = prod + pair_row(16 + h)
        logits = inner + LOGIT * pair_row(h) - coef[:, h : h + 1] * dist
        logits = jnp.where(valid, logits, -1000000000.0)
        peak = jnp.max(logits, axis=1, keepdims=True)
        e = jnp.exp(logits - peak)
        total = jnp.sum(e, axis=1, keepdims=True)
        upper = jnp.sum(e * prod, axis=1, keepdims=True)
        e_ref[h * rows : (h + 1) * rows, :] = e
        p_ref[h * rows : (h + 1) * rows, :] = prod
        d_ref[h * rows : (h + 1) * rows, :] = dist
        vec[h * rows : (h + 1) * rows, :] = jnp.where(
            lane == 0, peak, jnp.where(lane == 1, total, upper)
        )
    for b in range(H * rows // 128):
        stat_own[:, 128 * b : 128 * b + 128] = vec[128 * b : 128 * b + 128, :].T[0:8]

    pl.semaphore_wait(barrier, g1 - 1 + g2 - 1)

    stat_copies = []
    for d in range(1, cols_n):
        copy = pltpu.make_async_remote_copy(
            src_ref=stat_own,
            dst_ref=stat_in.at[d - 1],
            send_sem=stat_send.at[d - 1],
            recv_sem=stat_recv.at[d - 1],
            device_id=col_peer(d),
            device_id_type=MESH,
        )
        copy.start()
        stat_copies.append(copy)
    for copy in stat_copies:
        copy.wait()

    stats = [stat_own[...]] + [stat_in[d] for d in range(cols_n - 1)]
    peak = functools.reduce(jnp.maximum, [s[0:1] for s in stats])
    weights = [jnp.exp(s[0:1] - peak) for s in stats]
    total = sum(w * s[1:2] for w, s in zip(weights, stats))
    upper = sum(w * s[2:3] for w, s in zip(weights, stats))
    delta = upper / total
    scale = weights[0] / total
    eight = iota((8, 128), 0)
    for b in range(H * rows // 128):
        cut = slice(128 * b, 128 * b + 128)
        both = jnp.where(eight == 0, scale[:, cut], delta[:, cut])
        vec_t[cut, 0:8] = both.T

    kind = iota((32, 1), 0)
    is_vec = kind < 16
    is_point = (kind >= 16) & (kind < 28)
    head_sum = jnp.zeros((1, 128), F32)
    lane1 = iota((1, 128), 1)
    feat[816:KF, :] = jnp.zeros((KF - 816, cols), F32)
    for h in range(H):
        own = slice(h * rows, (h + 1) * rows)
        attn = e_ref[own, :] * vec_t[own, 0:1]
        dlog = attn * (p_ref[own, :] - vec_t[own, 1:2])
        moment = jnp.sum(jnp.sum(dlog * d_ref[own, :], axis=0, keepdims=True), axis=1, keepdims=True)
        head_sum = jnp.where(lane1 == h, moment, head_sum)
        put_pair_row(h, dlog)
        put_pair_row(16 + h, attn)
        e_ref[own, :] = attn
        p_ref[own, :] = dlog
        two = 2.0 * coef[:, h : h + 1]
        kd = dot3(split(q32[32 * h : 32 * h + 32, :]), split(dlog), 1, 0)
        col_sum = kd[29:30]
        kd = jnp.where(is_vec, kd, two * (kd - k32[32 * h : 32 * h + 32, :] * col_sum))
        ka = dot3(split(g48[48 * h : 48 * h + 48, :]), split(attn), 1, 0)
        feat[16 * h : 16 * h + 16, :] = kd[0:16]
        feat[VAL0 + 16 * h : VAL0 + 16 * h + 16, :] = ka[0:16]
        for x in range(3):
            at = KP0 + 48 * x + 4 * h
            feat[at : at + 4, :] = kd[16 + 4 * x : 20 + 4 * x]
            at = VP0 + 96 * x + 8 * h
            feat[at : at + 8, :] = ka[16 + 8 * x : 24 + 8 * x]
    share = kt.shape[2]
    for a in range(KF // 128):
        for b in range(cols // 128):
            block = feat[128 * a : 128 * a + 128, 128 * b : 128 * b + 128].T
            per = 128 // (share * n2)
            kt[b * per : (b + 1) * per, :, :, 128 * a : 128 * a + 128] = block.reshape(
                per, n2, share, 128
            )

    copy1 = pltpu.make_async_remote_copy(
        src_ref=kt.at[:, core_peer["row_2"]],
        dst_ref=k1,
        send_sem=k1_send,
        recv_sem=k1_recv,
        device_id=core_peer,
        device_id_type=MESH,
    )
    copy1.start()

    acc = jnp.zeros((16, CZ), F32)
    for i in range(rows):
        acc = acc + dot(pair_block(32 * i, 16).astype(BF), pair_v[i], 1, 0)
    w_own[...] = jnp.where(iota((16, 1), 0) == 12, head_sum, LOGIT * acc)
    w_copies = []
    for d in range(1, g1):
        copy = pltpu.make_async_remote_copy(
            src_ref=w_own,
            dst_ref=w_in.at[d - 1],
            send_sem=w_send.at[d - 1],
            recv_sem=w_recv.at[d - 1],
            device_id=one_peer(d),
            device_id_type=MESH,
        )
        copy.start()
        w_copies.append(copy)

    copy1.wait()
    p1[...] = (kt[:, i2] + k1[...]).reshape(p1.shape)
    copies2 = []
    for d in range(1, n1):
        y = lax.rem(i1 + d, n1)
        copy = pltpu.make_async_remote_copy(
            src_ref=p1.at[:, y],
            dst_ref=k2.at[d - 1],
            send_sem=k2_send.at[d - 1],
            recv_sem=k2_recv.at[d - 1],
            device_id={"row_1": y},
            device_id_type=MESH,
        )
        copy.start()
        copies2.append(copy)

    for h in range(H):
        own = slice(h * rows, (h + 1) * rows)
        two = 2.0 * coef[:, h : h + 1]
        qd = dot3(split(k32[32 * h : 32 * h + 32, :]), split(p_ref[own, :]), 1, 1)
        row_sum = qd[28:29]
        qd = jnp.where(is_vec, LOGIT * INNER * qd, two * (qd - q32[32 * h : 32 * h + 32, :] * row_sum))
        qa = dot3(split(v48[48 * h : 48 * h + 48, :]), split(e_ref[own, :]), 1, 1)
        qfeat[16 * h : 16 * h + 16, :] = qd[0:16]
        for x in range(3):
            at = 192 + 48 * x + 4 * h
            qfeat[at : at + 4, :] = qd[16 + 4 * x : 20 + 4 * x]
            at = 336 + 96 * x + 8 * h
            qfeat[at : at + 8, :] = qa[16 + 8 * x : 24 + 8 * x]
    qfeat[624:QF, :] = jnp.zeros((QF - 624, rows), F32)
    for a in range(QF // 128):
        qt[:, :, 128 * a : 128 * a + 128] = qfeat[128 * a : 128 * a + 128, :].T.reshape(
            qt.shape[0], qt.shape[1], 128
        )
    q_copies = []
    for d in range(1, cols_n):
        copy = pltpu.make_async_remote_copy(
            src_ref=qt.at[lax.rem(c + d, cols_n)],
            dst_ref=qin.at[d - 1],
            send_sem=q_send.at[d - 1],
            recv_sem=q_recv.at[d - 1],
            device_id=col_peer(d),
            device_id_type=MESH,
        )
        copy.start()
        q_copies.append(copy)

    w16s = (LOGIT * w16).astype(BF)
    zero32 = jnp.zeros((32, CZ), BF)
    stores = []
    for b in range(rows // 4):
        turned = pair_block(128 * b, 128).T.astype(BF)
        for half in range(2):
            first, second = 4 * b + 2 * half, 4 * b + 2 * half + 1
            wa = jnp.concatenate([w16s, stack(first)], axis=0)
            wb = jnp.concatenate([w16s, stack(second)], axis=0)
            left = [zero32] * 4
            right = [zero32] * 4
            left[2 * half], right[2 * half + 1] = wa, wb
            block = jnp.concatenate(
                [jnp.concatenate(left, axis=0), jnp.concatenate(right, axis=0)], axis=1
            )
            out = dot(turned, block, 1, 0)
            pg_v[first] = out[:, :CZ].astype(BF)
            pg_v[second] = out[:, CZ:].astype(BF)
        if (b + 1) % (rows // 4 // parts) == 0:
            p = (b + 1) // (rows // 4 // parts) - 1
            store = pltpu.make_async_copy(
                pg_v.at[pl.ds(p * step, step)], pg_hbm.at[pl.ds(p * step, step)], pg_sem.at[p]
            )
            store.start()
            stores.append(store)

    for copy in copies2:
        copy.wait()
    p2[...] = p1[:, i1] + functools.reduce(jnp.add, [k2[d] for d in range(n1 - 1)])
    copies3 = []
    for d in range(1, n0):
        z = lax.rem(i0 + d, n0)
        copy = pltpu.make_async_remote_copy(
            src_ref=p2.at[z],
            dst_ref=k3.at[d - 1],
            send_sem=k3_send.at[d - 1],
            recv_sem=k3_recv.at[d - 1],
            device_id={"row_0": z},
            device_id_type=MESH,
        )
        copy.start()
        copies3.append(copy)

    for copy in w_copies:
        copy.wait()
    w_mid[...] = w_own[...] + functools.reduce(jnp.add, [w_in[d] for d in range(g1 - 1)])
    w2_copies = []
    for d in range(1, g2):
        copy = pltpu.make_async_remote_copy(
            src_ref=w_mid,
            dst_ref=w_in2.at[d - 1],
            send_sem=w2_send.at[d - 1],
            recv_sem=w2_recv.at[d - 1],
            device_id=two_peer(d),
            device_id_type=MESH,
        )
        copy.start()
        w2_copies.append(copy)

    for copy in q_copies:
        copy.wait()
    query_out[...] = qt[c] + functools.reduce(jnp.add, [qin[d] for d in range(cols_n - 1)])
    for copy in copies3:
        copy.wait()
    key_out[...] = p2[i0] + functools.reduce(jnp.add, [k3[d] for d in range(n0 - 1)])
    for copy in w2_copies:
        copy.wait()
    small_out[...] = w_mid[...] + functools.reduce(jnp.add, [w_in2[d] for d in range(g2 - 1)])
    for store in stores:
        store.wait()


def finish_kernel(
    sizes,
    key_ref,
    query_ref,
    small_ref,
    hw_ref,
    qp_ref,
    kp_ref,
    vp_ref,
    rot_ref,
    trans_ref,
    gp_ref,
    qg_out,
    qpg_out,
    qfg_out,
    kg_out,
    vg_out,
    kpg_out,
    vpg_out,
    kfg_out,
    bw_out,
    hw_out,
):
    n0, n1, n2, m0, m1 = sizes
    share, qshare = key_ref.shape[0], query_ref.shape[0]
    rows, cols = gp_ref.shape[1], kp_ref.shape[2]
    i0, i1, i2 = (lax.axis_index(a) for a in ROW)
    j0, j1 = (lax.axis_index(a) for a in COL)
    r = (i0 * n1 + i1) * n2 + i2
    c = j0 * m1 + j1

    def pick(count, width, at):
        return (iota((count, width), 1) == iota((count, width), 0) + at).astype(F32)

    def take(sel, array):
        return dot(sel, array, 1, 1, HIGHEST)

    def frames(start, count):
        base = pl.multiple_of((start // 128) * 128, 128)
        sel = pick(count, 128, start - base)
        rot = [take(sel, rot_ref[x, :, pl.ds(base, 128)]) for x in range(3)]
        return rot, take(sel, trans_ref[:, pl.ds(base, 128)])

    def column(a, y):
        return a[:, y : y + 1]

    def total(a):
        return jnp.sum(a, axis=1, keepdims=True)

    def put_frame(out, parts):
        count = parts[0][0].shape[0]
        for x in range(3):
            lane = iota((count, 128), 1)
            wide = jnp.zeros((count, 128), F32)
            for y in range(4):
                wide = jnp.where(lane == y, parts[x][y], wide)
            if count % 8:
                wide = jnp.concatenate([wide, jnp.zeros((8 - count % 8, 128), F32)], axis=0)
            out[x] = wide.T[0:4, :count]

    rot, anchor = frames(r * rows + c * qshare, qshare)
    local_sel = pick(qshare, rows, c * qshare)
    summed = query_ref[...]
    qg_out[...] = summed[:, 0:192]
    dqg = [summed[:, 192 + 48 * x : 240 + 48 * x] for x in range(3)]
    opt = [summed[:, 336 + 96 * x : 432 + 96 * x] for x in range(3)]
    local = [take(local_sel, qp_ref[y]) for y in range(3)]
    cotan = [gp_ref[y, pl.ds(c * qshare, qshare), :] for y in range(3)]
    for y in range(3):
        qpg_out[y] = sum(column(rot[x], y) * dqg[x] for x in range(3))
    parts = []
    for x in range(3):
        shifted = opt[x] - column(anchor, x)
        turned = sum(column(rot[x], y) * cotan[y] for y in range(3))
        parts.append(
            [total(dqg[x] * local[y]) + total(shifted * cotan[y]) for y in range(3)]
            + [total(dqg[x]) - total(turned)]
        )
    put_frame(qfg_out, parts)

    rot, anchor = frames(c * cols + r * share, share)
    local_sel = pick(share, cols, r * share)
    summed = key_ref[...]
    kg_out[...] = summed[:, 0:192]
    vg_out[...] = summed[:, VAL0 : VAL0 + 192]
    dkg = [summed[:, KP0 + 48 * x : KP0 + 48 + 48 * x] for x in range(3)]
    dvg = [summed[:, VP0 + 96 * x : VP0 + 96 + 96 * x] for x in range(3)]
    klocal = [take(local_sel, kp_ref[y]) for y in range(3)]
    vlocal = [take(local_sel, vp_ref[y]) for y in range(3)]
    for y in range(3):
        kpg_out[y] = sum(column(rot[x], y) * dkg[x] for x in range(3))
        vpg_out[y] = sum(column(rot[x], y) * dvg[x] for x in range(3))
    parts = []
    for x in range(3):
        parts.append(
            [total(dkg[x] * klocal[y]) + total(dvg[x] * vlocal[y]) for y in range(3)]
            + [total(dkg[x]) + total(dvg[x])]
        )
    put_frame(kfg_out, parts)

    bw_out[...] = small_ref[0:H, :]
    raw = hw_ref[...]
    hw_out[...] = small_ref[12:13, 0:H] * (-0.5 * LOGIT * POINT) / (1.0 + jnp.exp(-raw))


def per_device(
    sizes,
    pair_rep,
    bias_weight,
    head_weight,
    queries,
    key_vectors,
    values,
    query_points,
    key_points,
    value_points,
    rotations,
    translations,
    residue_count,
    grad_output,
    grad_points,
    grad_pair,
):
    n0, n1, n2, m0, m1 = sizes
    cols_n, g1, g2 = m0 * m1, m0 * m1 * n2, n0 * n1
    rows, cols = pair_rep.shape[:2]
    share, qshare = cols // (n0 * n1 * n2), rows // cols_n
    head_row = head_weight.reshape(1, H)
    grad_points_t = jnp.transpose(grad_points, (0, 2, 1))
    vmem = pl.BlockSpec(memory_space=pltpu.VMEM)
    hbm = pl.BlockSpec(memory_space=pl.ANY)
    smem = pl.BlockSpec(memory_space=pltpu.SMEM)
    parts = 4

    def buf(*shape, dtype=F32):
        return pltpu.VMEM(shape, dtype)

    dma = pltpu.SemaphoreType.DMA
    pair_grad, key_sum, query_sum, small_sum = pl.pallas_call(
        functools.partial(tile_kernel, sizes),
        name="tile",
        out_shape=(
            jax.ShapeDtypeStruct(pair_rep.shape, BF),
            jax.ShapeDtypeStruct((share, KF), F32),
            jax.ShapeDtypeStruct((qshare, QF), F32),
            jax.ShapeDtypeStruct((16, CZ), F32),
        ),
        in_specs=[hbm] + [vmem] * 10 + [smem] + [vmem] * 3,
        out_specs=(hbm, vmem, vmem, vmem),
        scratch_shapes=[
            buf(rows, cols, CZ, dtype=BF),
            buf(rows, cols, CZ, dtype=BF),
            buf(cols // 128, rows * 32, 128),
            buf(H * rows, cols),
            buf(H * rows, cols),
            buf(H * rows, cols),
            buf(H * 32, rows),
            buf(H * 32, cols),
            buf(H * 48, rows),
            buf(H * 48, cols),
            buf(H * rows, 128),
            buf(H * rows, 128),
            buf(8, H * rows),
            buf(cols_n - 1, 8, H * rows),
            buf(KF, cols),
            buf(n0 * n1, n2, share, KF),
            buf(n0 * n1, share, KF),
            buf(n0, n1, share, KF),
            buf(n1 - 1, n0, share, KF),
            buf(n0, share, KF),
            buf(n0 - 1, share, KF),
            buf(QF, rows),
            buf(cols_n, qshare, QF),
            buf(cols_n - 1, qshare, QF),
            buf(16, CZ),
            buf(g1 - 1, 16, CZ),
            buf(16, CZ),
            buf(g2 - 1, 16, CZ),
            dma((parts,)),
            dma((parts,)),
            dma((cols_n - 1,)),
            dma((cols_n - 1,)),
            dma,
            dma,
            dma((n1 - 1,)),
            dma((n1 - 1,)),
            dma((n0 - 1,)),
            dma((n0 - 1,)),
            dma((cols_n - 1,)),
            dma((cols_n - 1,)),
            dma((g1 - 1,)),
            dma((g1 - 1,)),
            dma((g2 - 1,)),
            dma((g2 - 1,)),
        ],
        compiler_params=pltpu.CompilerParams(
            collective_id=0, has_side_effects=True, vmem_limit_bytes=48 * 1024 * 1024
        ),
    )(
        pair_rep,
        bias_weight.T,
        head_row,
        queries.T,
        key_vectors,
        values,
        query_points,
        key_points,
        value_points,
        rotations,
        translations,
        residue_count,
        grad_output.T,
        grad_points_t,
        jnp.transpose(grad_pair, (1, 0, 2)),
    )
    qg, qpg, qfg, kg, vg, kpg, vpg, kfg, bw, hw = pl.pallas_call(
        functools.partial(finish_kernel, sizes),
        name="finish",
        out_shape=(
            jax.ShapeDtypeStruct((qshare, 192), F32),
            jax.ShapeDtypeStruct((3, qshare, 48), F32),
            jax.ShapeDtypeStruct((3, 4, qshare), F32),
            jax.ShapeDtypeStruct((share, 192), F32),
            jax.ShapeDtypeStruct((share, 192), F32),
            jax.ShapeDtypeStruct((3, share, 48), F32),
            jax.ShapeDtypeStruct((3, share, 96), F32),
            jax.ShapeDtypeStruct((3, 4, share), F32),
            jax.ShapeDtypeStruct((H, CZ), F32),
            jax.ShapeDtypeStruct((1, H), F32),
        ),
        in_specs=[vmem] * 10,
        out_specs=(vmem,) * 10,
    )(
        key_sum,
        query_sum,
        small_sum,
        head_row,
        query_points,
        key_points,
        value_points,
        rotations,
        translations,
        grad_points_t,
    )

    def swap(a):
        return jnp.transpose(a, (0, 2, 1))

    return (
        pair_grad,
        qg.T,
        swap(qpg),
        qfg,
        kg.T,
        vg.T,
        swap(kpg),
        swap(vpg),
        kfg,
        bw.T,
        hw.reshape(H),
    )


def solution(mesh, sizes=(4, 4, 2, 4, 2)):
    finer = Mesh(mesh.devices.reshape(sizes), ROW_COL)
    in_specs = (
        P(ROW, COL, None),
        P(),
        P(),
        P(None, ROW),
        P(None, COL),
        P(None, COL),
        P(None, None, ROW),
        P(None, None, COL),
        P(None, None, COL),
        P(),
        P(),
        P(),
        P(None, ROW),
        P(None, None, ROW),
        P(ROW, None, None),
    )
    out_specs = (
        P(ROW, COL, None),
        P(None, ROW_COL),
        P(None, None, ROW_COL),
        P(None, None, ROW_COL),
        P(None, COL_ROW),
        P(None, COL_ROW),
        P(None, None, COL_ROW),
        P(None, None, COL_ROW),
        P(None, None, COL_ROW),
        P(),
        P(),
    )
    return jax.shard_map(
        functools.partial(per_device, sizes),
        mesh=finer,
        in_specs=in_specs,
        out_specs=out_specs,
        check_vma=False,
    )
```

time: 418 us -> 66.1 us (0.16)
  waiting for transfers between devices: 222 us -> 0 us
  blocking collectives: 48.8 us -> 0 us
  Pallas kernels: 0 us -> 44.6 us
  matrix products: 42.1 us -> 0 us
  starting transfers between devices: 31.5 us -> 0 us
  local copies, waits for them, and re-layouts: 45.3 us -> 19.5 us
  between operations: 16.3 us -> 1.33 us
  other arithmetic: 9.25 us -> 0 us
    unnamed x2 -> x0, waiting for transfers between devices: 206 us -> none
    psum x5 -> x0, blocking collectives: 48.8 us -> none  [by_axis(): return functools.reduce(lax.psum, axes, shard)]
    pallas_call x0 -> x2, Pallas kernels: none -> 44.6 us  [the longest x1 41.5 us: per_device(): pl.pallas_call(functools.partial(tile_kernel, sizes), name='tile', out_sh...]
    dot_general x27 -> x0, matrix products: 42.1 us -> none  [the longest x1 7.44 us: per_device(): jnp.einsum('hij,ihc->ijc', attn_rounded, grad_pair, preferred_element_typ...]
    all_to_all x4 -> x0, starting transfers between devices: 31.2 us -> none  [the longest x2 20.5 us: from_everyone(): lax.all_to_all(jnp.broadcast_to(shard[None], (count, *shard.shape)), axis...]
    all_to_all x4 -> x0, waiting for transfers between devices: 15.6 us -> none  [the longest x2 9.97 us: from_everyone(): lax.all_to_all(jnp.broadcast_to(shard[None], (count, *shard.shape)), axis...]
    another operation x6 -> x0, local copies, waits for them, and re-layouts: 8.47 us -> none  [split_up(): return jnp.moveaxis(shard.reshape(*before, count, -1, *after), dim, 0)]
    unnamed x96 -> x35, local copies, waits for them, and re-layouts: 11.8 us -> 19.5 us
  transfers between devices with their start and end apart: 5 -> 0, of which waited for: 3 -> 0; matrix products, arithmetic and copies ran while one was open for 11% -> 0% of each run, Pallas kernels for 0% -> 0%
where the time goes in v1:
time: 66.1 us; the launch traced here: 65.5 us
  Pallas kernels  44.6 us (67%)
  local copies, waits for them, and re-layouts  19.5 us (30%)
  between operations  1.33 us (2%)
    pallas_call x1, Pallas kernels, per_device(): pl.pallas_call(functools.partial(tile_kernel, sizes), name='tile', out_sh...  41.5 us
    unnamed x35, local copies, waits for them, and re-layouts  19.5 us
    pallas_call x1, Pallas kernels, per_device(): pl.pallas_call(functools.partial(finish_kernel, sizes), name='finish', ou...  3.06 us

profile of v1, /device:TPU:1, one launch (start us, length us, event | category | flops | bytes accessed | tf_op | source)
XLA Modules:
  0.0 65.5 jit_solution(14978504107385848476)
XLA Ops:
  1.3 0.0 copy-start.1
  1.3 1.0 %copy-done.1 = f32[3,96,256]{2,1,0:T(8,128)S(1)} copy-done((f32[3,96,256]{2,1,0:T(8,128)S(1)}, f32[3,96,256]{2,1,0:T(8,128)}, u32[]{:S(2)}) %copy-start.1) | copy-done | bytes 294936
  2.3 0.0 copy-start.2
  2.3 0.9 %copy-done.2 = f32[3,48,256]{2,1,0:T(8,128)S(1)} copy-done((f32[3,48,256]{2,1,0:T(8,128)S(1)}, f32[3,48,256]{2,1,0:T(8,128)}, u32[]{:S(2)}) %copy-start.2) | copy-done | bytes 147480
  3.2 0.0 copy-start.3
  3.2 0.9 %copy-done.3 = f32[3,3,2048]{2,1,0:T(4,128)S(1)} copy-done((f32[3,3,2048]{2,1,0:T(4,128)S(1)}, f32[3,3,2048]{2,1,0:T(4,128)}, u32[]{:S(2)}) %copy-start.3) | copy-done | bytes 73752
  4.1 0.0 copy-start.4
  4.1 0.9 %copy-done.4 = f32[3,96,64]{1,2,0:T(8,128)S(1)} copy-done((f32[3,96,64]{1,2,0:T(8,128)S(1)}, f32[3,96,64]{1,2,0:T(8,128)}, u32[]{:S(2)}) %copy-start.4) | copy-done | bytes 73752
  5.0 0.0 copy-start.5
  5.0 0.9 %copy-done.5 = f32[3,48,64]{2,1,0:T(8,128)S(1)} copy-done((f32[3,48,64]{2,1,0:T(8,128)S(1)}, f32[3,48,64]{2,1,0:T(8,128)}, u32[]{:S(2)}) %copy-start.5) | copy-done | bytes 36888
  5.8 0.0 copy-start.6
  5.8 0.9 %copy-done.6 = f32[192,256]{1,0:T(8,128)S(1)} copy-done((f32[192,256]{1,0:T(8,128)S(1)}, f32[192,256]{1,0:T(8,128)}, u32[]{:S(2)}) %copy-start.6) | copy-done | bytes 196632
  6.8 0.0 copy-start.7
  6.8 0.9 %copy-done.7 = f32[192,256]{1,0:T(8,128)S(1)} copy-done((f32[192,256]{1,0:T(8,128)S(1)}, f32[192,256]{1,0:T(8,128)}, u32[]{:S(2)}) %copy-start.7) | copy-done | bytes 196632
  7.7 0.0 copy-start.8
  7.7 0.9 %copy-done.8 = bf16[64,12,128]{2,0,1:T(8,128)(2,1)S(1)} copy-done((bf16[64,12,128]{2,0,1:T(8,128)(2,1)S(1)}, bf16[64,12,128]{2,0,1:T(8,128)(2,1)}, u32[]{:S(2)}) %copy-start.8) | copy-done | bytes 196632
  8.6 0.0 copy-start.9
  8.6 0.8 %copy-done.9 = f32[3,2048]{1,0:T(4,128)S(1)} copy-done((f32[3,2048]{1,0:T(4,128)S(1)}, f32[3,2048]{1,0:T(4,128)}, u32[]{:S(2)}) %copy-start.9) | copy-done | bytes 24600
  9.4 0.0 copy-start.10
  9.4 0.8 %copy-done.10 = f32[192,64]{0,1:T(8,128)S(1)} copy-done((f32[192,64]{0,1:T(8,128)S(1)}, f32[192,64]{0,1:T(8,128)}, u32[]{:S(2)}) %copy-start.10) | copy-done | bytes 49176
  10.2 0.0 copy-start.11
  10.2 0.8 %copy-done.11 = f32[192,64]{0,1:T(8,128)S(1)} copy-done((f32[192,64]{0,1:T(8,128)S(1)}, f32[192,64]{0,1:T(8,128)}, u32[]{:S(2)}) %copy-start.11) | copy-done | bytes 49176
  11.1 0.0 copy-start.15
  11.1 0.7 %copy-done.15 = bf16[128,12]{0,1:T(8,128)(2,1)S(1)} copy-done((bf16[128,12]{0,1:T(8,128)(2,1)S(1)}, bf16[128,12]{0,1:T(8,128)(2,1)}, u32[]{:S(2)}) %copy-start.15) | copy-done | bytes 3096
  11.7 0.0 copy-start.16
  11.7 0.7 copy-done.16
  12.4 41.5 %tile.1 = (bf16[64,256,128]{2,1,0:T(8,128)(2,1)S(1)}, f32[8,896]{1,0:T(8,128)S(1)}, f32[8,768]{1,0:T(8,128)S(1)}, f32[16,128]{1,0:T(8,128)S(1)}) custom-call(bf16[64,256,128]{2,1,0:T(8,128)(2,1)} %pair_hbm.1, bf16[12,128]{1,0:T(8,128)(2,1)S(1)} %bitcast.19, f32[1,12]{1,0:T(1,128)S(1)} %bitcast.21, f32[64,192]{1,0:T(8,128)S(1)} %bitcast.17, ...), custom_call_target="tpu_custom_call" | custom-call | tf_op jit(solution)/shard_map/tile/pallas_call | solution.py:628
  54.0 0.0 copy-start
  54.0 1.9 %copy-done = bf16[64,256,128]{2,1,0:T(8,128)(2,1)} copy-done((bf16[64,256,128]{2,1,0:T(8,128)(2,1)}, bf16[64,256,128]{2,1,0:T(8,128)(2,1)S(1)}, u32[]{:S(2)}) %copy-start) | copy-done | bytes 4194328
  55.9 0.0 copy-start.12
  55.9 0.6 copy-done.12
  56.5 0.0 copy-start.13
  56.5 0.6 copy-done.13
  57.1 0.0 copy-start.14
  57.1 0.6 copy-done.14
  57.7 3.1 %finish.1 = (f32[8,192]{1,0:T(8,128)}, f32[3,8,48]{2,1,0:T(8,128)}, f32[3,4,8]{2,1,0:T(4,128)}, f32[8,192]{1,0:T(8,128)}, f32[8,192]{1,0:T(8,128)}, /*index=5*/f...) custom-call(f32[8,896]{1,0:T(8,128)} %copy-done.12, ...), custom_call_target="tpu_custom_call" | custom-call | tf_op jit(solution)/shard_map/finish/pallas_call | solution.py:705
  60.8 4.7 %copy.28 = bf16[64,256,128]{2,1,0:T(8,128)(2,1)} copy(bf16[64,256,128]{2,1,0:T(8,128)(2,1)} %copy-done) | data formatting | bytes 8388608
Async XLA Ops:
  1.3 1.0 %copy-start.1 = (f32[3,96,256]{2,1,0:T(8,128)S(1)}, f32[3,96,256]{2,1,0:T(8,128)}, u32[]{:S(2)}) copy-start(f32[3,96,256]{2,1,0:T(8,128)} %vp_ref.3) | copy-start | bytes 884740
  2.3 0.9 %copy-start.2 = (f32[3,48,256]{2,1,0:T(8,128)S(1)}, f32[3,48,256]{2,1,0:T(8,128)}, u32[]{:S(2)}) copy-start(f32[3,48,256]{2,1,0:T(8,128)} %kp_ref.3) | copy-start | bytes 442372
  3.2 0.9 %copy-start.3 = (f32[3,3,2048]{2,1,0:T(4,128)S(1)}, f32[3,3,2048]{2,1,0:T(4,128)}, u32[]{:S(2)}) copy-start(f32[3,3,2048]{2,1,0:T(4,128)} %rot_ref.3) | copy-start | bytes 221188
  4.1 0.9 %copy-start.4 = (f32[3,96,64]{1,2,0:T(8,128)S(1)}, f32[3,96,64]{1,2,0:T(8,128)}, u32[]{:S(2)}) copy-start(f32[3,96,64]{1,2,0:T(8,128)} %param.28) | copy-start | bytes 221188
  5.0 0.9 %copy-start.5 = (f32[3,48,64]{2,1,0:T(8,128)S(1)}, f32[3,48,64]{2,1,0:T(8,128)}, u32[]{:S(2)}) copy-start(f32[3,48,64]{2,1,0:T(8,128)} %qp_ref.3) | copy-start | bytes 110596
  5.8 0.9 %copy-start.6 = (f32[192,256]{1,0:T(8,128)S(1)}, f32[192,256]{1,0:T(8,128)}, u32[]{:S(2)}) copy-start(f32[192,256]{1,0:T(8,128)} %k_ref.1) | copy-start | bytes 589828
  6.8 0.9 %copy-start.7 = (f32[192,256]{1,0:T(8,128)S(1)}, f32[192,256]{1,0:T(8,128)}, u32[]{:S(2)}) copy-start(f32[192,256]{1,0:T(8,128)} %v_ref.1) | copy-start | bytes 589828
  7.7 0.9 %copy-start.8 = (bf16[64,12,128]{2,0,1:T(8,128)(2,1)S(1)}, bf16[64,12,128]{2,0,1:T(8,128)(2,1)}, u32[]{:S(2)}) copy-start(bf16[64,12,128]{2,0,1:T(8,128)(2,1)} %param.29) | copy-start | bytes 589828
  8.6 0.8 %copy-start.9 = (f32[3,2048]{1,0:T(4,128)S(1)}, f32[3,2048]{1,0:T(4,128)}, u32[]{:S(2)}) copy-start(f32[3,2048]{1,0:T(4,128)} %trans_ref.3) | copy-start | bytes 73732
  9.4 0.8 %copy-start.10 = (f32[192,64]{0,1:T(8,128)S(1)}, f32[192,64]{0,1:T(8,128)}, u32[]{:S(2)}) copy-start(f32[192,64]{0,1:T(8,128)} %param.18) | copy-start | bytes 147460
  10.2 0.8 %copy-start.11 = (f32[192,64]{0,1:T(8,128)S(1)}, f32[192,64]{0,1:T(8,128)}, u32[]{:S(2)}) copy-start(f32[192,64]{0,1:T(8,128)} %param.27) | copy-start | bytes 147460
  11.1 0.7 %copy-start.15 = (bf16[128,12]{0,1:T(8,128)(2,1)S(1)}, bf16[128,12]{0,1:T(8,128)(2,1)}, u32[]{:S(2)}) copy-start(bf16[128,12]{0,1:T(8,128)(2,1)} %param.16) | copy-start | bytes 9220
  11.7 0.7 %copy-start.16 = (f32[12]{0:T(128)S(1)}, f32[12]{0:T(128)}, u32[]{:S(2)}) copy-start(f32[12]{0:T(128)} %param.17) | copy-start | bytes 148
  54.0 2.0 %copy-start = (bf16[64,256,128]{2,1,0:T(8,128)(2,1)}, bf16[64,256,128]{2,1,0:T(8,128)(2,1)S(1)}, u32[]{:S(2)}) copy-start(bf16[64,256,128]{2,1,0:T(8,128)(2,1)S(1)} %get-tuple-element.50) | copy-start | bytes 12582916
  55.9 0.6 copy-start.12
  56.5 0.6 copy-start.13
  57.1 0.6 copy-start.14

commit v2 on v1

v2 whole, which is shorter than its diff:
```python
import functools
import math

import jax
import jax.numpy as jnp
from jax import lax
from jax.experimental import pallas as pl
from jax.experimental.pallas import tpu as pltpu
from jax.sharding import Mesh
from jax.sharding import PartitionSpec as P

ROW = ("row_0", "row_1", "row_2")
COL = ("col_0", "col_1")
ROW_COL = ROW + COL
COL_ROW = COL + ROW

H, C, PQ, PV, CZ = 12, 16, 4, 8, 128
KD, KV, QF = 384, 512, 640
LOGIT = math.sqrt(1.0 / 3.0)
POINT = math.sqrt(2.0 / (9.0 * PQ))
INNER = 1.0 / math.sqrt(C)

F32, BF = jnp.float32, jnp.bfloat16
HIGHEST = lax.Precision.HIGHEST
MESH = pl.DeviceIdType.MESH
VMEM_BYTES = 67043328


def dot(a, b, ca, cb, precision=None):
    return lax.dot_general(
        a, b, (((ca,), (cb,)), ((), ())), precision=precision, preferred_element_type=F32
    )


def split(a):
    hi = a.astype(BF)
    return hi, (a - hi.astype(F32)).astype(BF)


def dot3(a, b, ca, cb):
    (ah, al), (bh, bl) = a, b
    return dot(ah, bh, ca, cb) + dot(ah, bl, ca, cb) + dot(al, bh, ca, cb)


def split3(a):
    first = a.astype(BF)
    rest = a - first.astype(F32)
    second = rest.astype(BF)
    return first, second, (rest - second.astype(F32)).astype(BF)


def dot6(a, b):
    (a1, a2, a3), (b1, b2, b3) = split3(a), split3(b)
    left = jnp.concatenate([a1, a1, a1, a2, a2, a3], axis=0)
    return dot(left, jnp.concatenate([b1, b2, b3, b1, b2, b1], axis=0), 0, 0)


def three(a, axis):
    hi, lo = split(a)
    return jnp.concatenate([hi, hi, lo], axis=axis)


def three_rhs(b):
    hi, lo = split(b)
    return jnp.concatenate([hi, lo, hi], axis=0)


def iota(shape, dim):
    return lax.broadcasted_iota(jnp.int32, shape, dim)


def softplus(x):
    return jnp.maximum(x, 0.0) + jnp.log1p(jnp.exp(-jnp.abs(x)))


def tile_kernel(
    sizes,
    pair_hbm,
    *refs,
):
    inputs, refs = refs[:14], refs[14:]
    sums, refs = refs[:5], refs[5:]
    copies_in, refs = refs[:14], refs[14:]
    tile_body(sizes, pair_hbm, inputs, copies_in, *sums, *copies_in, *refs)


def tile_body(
    sizes,
    pair_hbm,
    inputs,
    copies_in,
    turn_hbm,
    kd_hbm,
    kv_hbm,
    query_hbm,
    small_hbm,
    wt_ref,
    hw_ref,
    q_ref,
    k_ref,
    v_ref,
    qp_ref,
    kp_ref,
    vp_ref,
    rot_ref,
    trans_ref,
    count_ref,
    go_ref,
    gp_ref,
    gpair_ref,
    pair_v,
    turn_v,
    kd_out,
    kv_out,
    query_out,
    small_out,
    s_ref,
    e_ref,
    p_ref,
    d_ref,
    q32,
    k32,
    g48,
    v48,
    vec,
    own_peak,
    stat_own,
    stat_in,
    q_pack,
    g_pack,
    qa,
    qb,
    qv,
    qfeat,
    qt,
    qx,
    qy,
    qz,
    kd_refs,
    kv_refs,
    w_refs,
    in_sem,
    pair_sem,
    out_sem,
    stat_sems,
    qx_sems,
    qz_sems,
    kd_sems,
    kv_sems,
    w_sems,
):
    n0, n1, n2, m0, m1 = sizes
    cols_n = m0 * m1
    rows = q_ref.shape[0]
    cols = k_ref.shape[1]
    i0, i1, i2 = (lax.axis_index(a) for a in ROW)
    j0, j1 = (lax.axis_index(a) for a in COL)
    r = (i0 * n1 + i1) * n2 + i2
    c = j0 * m1 + j1

    def col_peer(d):
        p = lax.rem(c + d, cols_n)
        return {"col_0": p // m1, "col_1": lax.rem(p, m1)}

    groups = {
        "z": (m1 * n0, j1 * n0 + i0, lambda p: {"col_1": p // n0, "row_0": lax.rem(p, n0)}),
        "x": (m0 * n2, j0 * n2 + i2, lambda p: {"col_0": p // n2, "row_2": lax.rem(p, n2)}),
        "y": (n1, i1, lambda p: {"row_1": p}),
    }

    def group_peer(name, d):
        count, here, place = groups[name]
        return place(lax.rem(here + d, count))

    def send(src, dst, sems, n, device):
        copy = pltpu.make_async_remote_copy(
            src_ref=src,
            dst_ref=dst,
            send_sem=sems[0].at[n],
            recv_sem=sems[1].at[n],
            device_id=device,
            device_id_type=MESH,
        )
        copy.start()
        return copy

    parts = pair_sem.shape[0]
    step = rows // parts
    loads = [
        pltpu.make_async_copy(
            pair_hbm.at[pl.ds(b * step, step)], pair_v.at[pl.ds(b * step, step)], pair_sem.at[b]
        )
        for b in range(parts)
    ]
    smalls = [
        pltpu.make_async_copy(src, dst, in_sem.at[n])
        for n, (src, dst) in enumerate(zip(inputs, copies_in))
    ]
    for load in smalls:
        load.start()

    barrier = pltpu.get_barrier_semaphore()
    expected = 0
    for d in range(1, cols_n):
        pl.semaphore_signal(barrier, inc=1, device_id=col_peer(d), device_id_type=MESH)
        expected += 1
    for name in groups:
        for d in range(1, groups[name][0]):
            pl.semaphore_signal(
                barrier, inc=1, device_id=group_peer(name, d), device_id_type=MESH
            )
            expected += 1

    for load in loads:
        load.start()
    for load in smalls:
        load.wait()

    col_start = pl.multiple_of(c * cols, 128)
    row_start = r * rows
    row_base = pl.multiple_of((row_start // 128) * 128, 128)
    row_half = lax.rem(row_start, 128)

    def row_window(w):
        return jnp.where(row_half == 0, w[:, :rows], w[:, 128 - rows :])

    def row_rot(x, y):
        return row_window(rot_ref[x, pl.ds(y, 1), pl.ds(row_base, 128)])

    def col_rot(x, y):
        return rot_ref[x, pl.ds(y, 1), pl.ds(col_start, cols)]

    coef = 0.5 * LOGIT * POINT * softplus(hw_ref[...])

    zero_q = jnp.zeros((2, rows), F32)
    zero_k = jnp.zeros((2, cols), F32)
    q_t = q_ref[...].T * (LOGIT * INNER)
    k_all = k_ref[...]
    rr = [[row_rot(x, y) for y in range(3)] for x in range(3)]
    cr = [[col_rot(x, y) for y in range(3)] for x in range(3)]
    for x in range(3):
        t_row = row_window(trans_ref[pl.ds(x, 1), pl.ds(row_base, 128)])
        t_col = trans_ref[pl.ds(x, 1), pl.ds(col_start, cols)]
        qg = sum(rr[x][y] * qp_ref[y] for y in range(3)) + t_row
        kg = sum(cr[x][y] * kp_ref[y] for y in range(3)) + t_col
        vg = sum(cr[x][y] * vp_ref[y] for y in range(3)) + t_col
        for h in range(H):
            q32[32 * h + 16 + 4 * x : 32 * h + 20 + 4 * x, :] = qg[4 * h : 4 * h + 4]
            k32[32 * h + 16 + 4 * x : 32 * h + 20 + 4 * x, :] = kg[4 * h : 4 * h + 4]
            v48[48 * h + 16 + 8 * x : 48 * h + 24 + 8 * x, :] = vg[8 * h : 8 * h + 8]
    gp_t = [gp_ref[y].T for y in range(3)]
    for x in range(3):
        gg = sum(rr[x][y] * gp_t[y] for y in range(3))
        for h in range(H):
            g48[48 * h + 16 + 8 * x : 48 * h + 24 + 8 * x, :] = gg[8 * h : 8 * h + 8]
    go_t = go_ref[...].T
    for h in range(H):
        q32[32 * h : 32 * h + 16, :] = q_t[16 * h : 16 * h + 16]
        k32[32 * h : 32 * h + 16, :] = k_all[16 * h : 16 * h + 16]
        g48[48 * h : 48 * h + 16, :] = go_t[16 * h : 16 * h + 16]
        v48[48 * h : 48 * h + 16, :] = v_ref[16 * h : 16 * h + 16, :]
        g48[48 * h + 40 : 48 * h + 48, :] = jnp.zeros((8, rows), F32)
        v48[48 * h + 40 : 48 * h + 48, :] = jnp.zeros((8, cols), F32)
        qh = q32[32 * h + 16 : 32 * h + 28, :]
        kh = k32[32 * h + 16 : 32 * h + 28, :]
        q32[32 * h + 28 : 32 * h + 32, :] = jnp.concatenate(
            [jnp.sum(qh * qh, axis=0, keepdims=True), jnp.ones((1, rows), F32), zero_q], axis=0
        )
        k32[32 * h + 28 : 32 * h + 32, :] = jnp.concatenate(
            [jnp.ones((1, cols), F32), jnp.sum(kh * kh, axis=0, keepdims=True), zero_k], axis=0
        )

    def pair_row(at):
        return jnp.concatenate(
            [s_ref[a, pl.ds(at, rows, stride=32), :] for a in range(cols // 128)], axis=1
        )

    def put_pair_row(at, value):
        for a in range(cols // 128):
            s_ref[a, pl.ds(at, rows, stride=32), :] = value[:, 128 * a : 128 * a + 128]

    def pair_block(at, count):
        return jnp.concatenate(
            [s_ref[a, at : at + count, :] for a in range(cols // 128)], axis=1
        )

    w16 = jnp.concatenate([wt_ref[...].astype(F32), jnp.zeros((4, CZ), F32)], axis=0)
    w16b = w16.astype(BF)

    def stack(i):
        gpad = jnp.concatenate(
            [gpair_ref[:, i, :].astype(F32), jnp.zeros((4, CZ), F32)], axis=0
        ).astype(BF)
        return gpad

    point_row = iota((16, 1), 0) < 12
    for h in range(H):
        own = slice(h * rows, (h + 1) * rows)
        kb = k32[32 * h + 16 : 32 * h + 32, :]
        inner = dot6(q32[32 * h : 32 * h + 16, :], k32[32 * h : 32 * h + 16, :])
        dist = dot6(q32[32 * h + 16 : 32 * h + 32, :], jnp.where(point_row, -2.0 * kb, kb))
        d_ref[own, :] = dist
        e_ref[own, :] = inner - coef[:, h : h + 1] * dist
        p_ref[own, :] = dot(
            three(g48[48 * h : 48 * h + 48, :], 0), three_rhs(v48[48 * h : 48 * h + 48, :]), 0, 0
        )

    for b in range(parts):
        loads[b].wait()
        for ii in range(step):
            i = b * step + ii
            both = jnp.concatenate([w16b, stack(i)], axis=0)
            proj = dot(both, pair_v[i], 1, 1)
            for a in range(cols // 128):
                s_ref[a, 32 * i : 32 * i + 32, :] = proj[:, 128 * a : 128 * a + 128]

    valid = col_start + iota((1, cols), 1) < count_ref[0]
    lane = iota((rows, 128), 1)
    for h in range(H):
        own = slice(h * rows, (h + 1) * rows)
        prod = p_ref[own, :] + pair_row(16 + h)
        logits = e_ref[own, :] + LOGIT * pair_row(h)
        logits = jnp.where(valid, logits, -1000000000.0)
        peak = jnp.max(logits, axis=1, keepdims=True)
        e = jnp.exp(logits - peak)
        total = jnp.sum(e, axis=1, keepdims=True)
        upper = jnp.sum(e * prod, axis=1, keepdims=True)
        e_ref[own, :] = e
        p_ref[own, :] = prod
        vec[h * rows : (h + 1) * rows, :] = jnp.where(
            lane == 0, peak + jnp.log(total), jnp.where(lane == 1, upper / total, peak)
        )
    blocks = H * rows // 128
    stat_own[...] = jnp.zeros_like(stat_own)
    own_peak[...] = jnp.zeros_like(own_peak)
    for b in range(blocks):
        turned = vec[128 * b : 128 * b + 128, :].T
        stat_own[b : b + 1, :] = turned[0:1]
        stat_own[8 + b : 9 + b, :] = turned[1:2]
        own_peak[b : b + 1, :] = turned[2:3]

    pl.semaphore_wait(barrier, expected)

    stat_copies = [
        send(stat_own, stat_in.at[d - 1], stat_sems, d - 1, col_peer(d)) for d in range(1, cols_n)
    ]

    for h in range(H):
        own = slice(h * rows, (h + 1) * rows)
        e = e_ref[own, :]
        es = split(e)
        ks = split(k32[32 * h : 32 * h + 32, :])
        qa[32 * h : 32 * h + 32, :] = dot3(ks, split(e * (p_ref[own, :] - vec[own, 1:2])), 1, 1)
        qb[32 * h : 32 * h + 32, :] = dot3(ks, es, 1, 1)
        qv[24 * h : 24 * h + 24, :] = dot3(split(v48[48 * h : 48 * h + 48, :]), es, 1, 1)[16:40]

    for h in range(H):
        q_pack[32 * h : 32 * h + 32, :] = three(q32[32 * h : 32 * h + 32, :], 1)
        g_pack[48 * h : 48 * h + 48, :] = three(g48[48 * h : 48 * h + 48, :], 1)

    for copy in stat_copies:
        copy.wait()

    stats = [stat_own[...]] + [stat_in[d] for d in range(cols_n - 1)]
    peak = functools.reduce(jnp.maximum, [s[0:8] for s in stats])
    weights = [jnp.exp(s[0:8] - peak) for s in stats]
    total = functools.reduce(jnp.add, weights)
    delta = functools.reduce(jnp.add, [w * s[8:16] for w, s in zip(weights, stats)]) / total
    scale = jnp.exp(own_peak[...] - peak) / total
    shift = delta - stats[0][8:16]
    scale_t, delta_t = scale.T, delta.T

    kind = iota((32, 1), 0)
    is_vec = kind < 16

    class Staged:
        def __init__(self, refs, sems, out):
            self.feat, self.kt, self.k1, self.p1, self.k2, self.p2, self.k3 = refs
            self.sems = (sems[0:2], sems[2:4], sems[4:6])
            self.out = out

        def turn(self):
            share = self.kt.shape[2]
            per = 128 // (share * n2)
            for a in range(self.feat.shape[0] // 128):
                for b in range(cols // 128):
                    block = self.feat[128 * a : 128 * a + 128, 128 * b : 128 * b + 128].T
                    self.kt[b * per : (b + 1) * per, :, :, 128 * a : 128 * a + 128] = block.reshape(
                        per, n2, share, 128
                    )

        def send1(self):
            other = lax.rem(i2 + 1, n2)
            self.copies = [send(self.kt.at[:, other], self.k1, self.sems[0], 0, {"row_2": other})]

        def wait(self):
            for copy in self.copies:
                copy.wait()

        def send2(self):
            self.wait()
            self.p1[...] = (self.kt[:, i2] + self.k1[...]).reshape(self.p1.shape)
            self.copies = []
            for d in range(1, n1):
                to = lax.rem(i1 + d, n1)
                self.copies.append(
                    send(self.p1.at[:, to], self.k2.at[d - 1], self.sems[1], d - 1, {"row_1": to})
                )

        def send3(self):
            self.wait()
            self.p2[...] = self.p1[:, i1] + functools.reduce(
                jnp.add, [self.k2[d] for d in range(n1 - 1)]
            )
            self.copies = []
            for d in range(1, n0):
                to = lax.rem(i0 + d, n0)
                self.copies.append(
                    send(self.p2.at[to], self.k3.at[d - 1], self.sems[2], d - 1, {"row_0": to})
                )

        def finish(self):
            self.wait()
            self.out[...] = self.p2[i0] + functools.reduce(
                jnp.add, [self.k3[d] for d in range(n0 - 1)]
            )

    side_d = Staged(kd_refs, kd_sems, kd_out)
    side_v = Staged(kv_refs, kv_sems, kv_out)

    head_sum = jnp.zeros((1, 128), F32)
    lane1 = iota((1, 128), 1)
    side_d.feat[336:KD, :] = jnp.zeros((KD - 336, cols), F32)
    side_v.feat[480:KV, :] = jnp.zeros((KV - 480, cols), F32)
    for h in range(H):
        own = slice(h * rows, (h + 1) * rows)
        at = (slice(rows * (h % 2), rows * (h % 2) + rows), slice(h // 2, h // 2 + 1))
        attn = e_ref[own, :] * scale_t[at]
        dlog = attn * (p_ref[own, :] - delta_t[at])
        moment = jnp.sum(jnp.sum(dlog * d_ref[own, :], axis=0, keepdims=True), axis=1, keepdims=True)
        head_sum = jnp.where(lane1 == h, moment, head_sum)
        put_pair_row(h, dlog)
        put_pair_row(16 + h, attn)
        e_ref[own, :] = attn
        two = 2.0 * coef[:, h : h + 1]
        kd = dot(q_pack[32 * h : 32 * h + 32, :], three_rhs(dlog), 1, 0)
        col_sum = kd[29:30]
        kd = jnp.where(is_vec, kd, two * (kd - k32[32 * h : 32 * h + 32, :] * col_sum))
        side_d.feat[16 * h : 16 * h + 16, :] = kd[0:16]
        for x in range(3):
            to = 192 + 48 * x + 4 * h
            side_d.feat[to : to + 4, :] = kd[16 + 4 * x : 20 + 4 * x]
    side_d.turn()
    side_d.send1()

    for h in range(H):
        own = slice(h * rows, (h + 1) * rows)
        ka = dot(g_pack[48 * h : 48 * h + 48, :], three_rhs(e_ref[own, :]), 1, 0)
        side_v.feat[16 * h : 16 * h + 16, :] = ka[0:16]
        for x in range(3):
            to = 192 + 96 * x + 8 * h
            side_v.feat[to : to + 8, :] = ka[16 + 8 * x : 24 + 8 * x]
    side_v.turn()
    side_v.send1()

    acc = jnp.zeros((16, CZ), F32)
    for i in range(rows):
        acc = acc + dot(pair_block(32 * i, 16).astype(BF), pair_v[i], 1, 0)

    class Small:
        def __init__(self, value):
            w_refs[0][...] = value
            self.level = 0

        def send(self, name):
            at = self.level
            self.copies = [
                send(
                    w_refs[2 * at],
                    w_refs[2 * at + 1].at[d - 1],
                    w_sems[2 * at : 2 * at + 2],
                    d - 1,
                    group_peer(name, d),
                )
                for d in range(1, groups[name][0])
            ]

        def add(self):
            for copy in self.copies:
                copy.wait()
            here, came = w_refs[2 * self.level], w_refs[2 * self.level + 1]
            total = here[...] + functools.reduce(
                jnp.add, [came[d] for d in range(came.shape[0])]
            )
            self.level += 1
            if self.level < 3:
                w_refs[2 * self.level][...] = total
            return total

    small = Small(jnp.where(iota((16, 1), 0) == 12, head_sum, LOGIT * acc))
    small.send("z")

    side_d.send2()

    for h in range(H):
        at = (slice(h // 2, h // 2 + 1), slice(rows * (h % 2), rows * (h % 2) + rows))
        two = 2.0 * coef[:, h : h + 1]
        head = slice(32 * h, 32 * h + 32)
        qd = scale[at] * (qa[head, :] - shift[at] * qb[head, :])
        row_sum = qd[28:29]
        qd = jnp.where(is_vec, LOGIT * INNER * qd, two * (qd - q32[head, :] * row_sum))
        opt = scale[at] * qv[24 * h : 24 * h + 24, :]
        qfeat[16 * h : 16 * h + 16, :] = qd[0:16]
        for x in range(3):
            to = 192 + 48 * x + 4 * h
            qfeat[to : to + 4, :] = qd[16 + 4 * x : 20 + 4 * x]
            to = 336 + 96 * x + 8 * h
            qfeat[to : to + 8, :] = opt[8 * x : 8 * x + 8]
    qfeat[624:QF, :] = jnp.zeros((QF - 624, rows), F32)
    for a in range(QF // 128):
        qt[:, :, 128 * a : 128 * a + 128] = qfeat[128 * a : 128 * a + 128, :].T.reshape(
            qt.shape[0], qt.shape[1], 128
        )
    qx_copies = []
    for d in range(1, m0):
        to = lax.rem(j0 + d, m0)
        qx_copies.append(
            send(qt.at[pl.ds(to * m1, m1)], qx.at[d - 1], qx_sems, d - 1, {"col_0": to})
        )

    side_v.send2()

    for b in range(rows // 4):
        turn_v[b] = pair_block(128 * b, 128).T.astype(BF)
    turn_copy = pltpu.make_async_copy(turn_v, turn_hbm, out_sem.at[0])
    turn_copy.start()

    small.add()
    small.send("x")
    side_d.send3()
    for copy in qx_copies:
        copy.wait()
    qy[...] = qt[pl.ds(j0 * m1, m1)] + functools.reduce(jnp.add, [qx[d] for d in range(m0 - 1)])
    qz_copies = []
    for d in range(1, m1):
        to = lax.rem(j1 + d, m1)
        qz_copies.append(send(qy.at[to], qz.at[d - 1], qz_sems, d - 1, {"col_1": to}))
    side_v.send3()
    small.add()
    small.send("y")
    side_d.finish()
    side_v.finish()
    for copy in qz_copies:
        copy.wait()
    query_out[...] = functools.reduce(jnp.add, [qz[d] for d in range(m1 - 1)], qy[j1])
    small_out[...] = small.add()
    outs = [
        pltpu.make_async_copy(query_out, query_hbm, out_sem.at[1]),
        pltpu.make_async_copy(kd_out, kd_hbm, out_sem.at[2]),
        pltpu.make_async_copy(kv_out, kv_hbm, out_sem.at[3]),
        pltpu.make_async_copy(small_out, small_hbm, out_sem.at[4]),
    ]
    for copy in outs:
        copy.start()
    for copy in outs + [turn_copy]:
        copy.wait()


def finish_kernel(sizes, *refs):
    inputs, refs = refs[:14], refs[14:]
    outs, refs = refs[:11], refs[11:]
    copies_in, refs = refs[:14], refs[14:]
    results, (pg_v, in_sem, pg_sem, out_sem) = refs[:10], refs[10:]
    turn_ref, wt_ref, gpair_ref = copies_in[:3]
    loads = [
        pltpu.make_async_copy(src, dst, in_sem.at[n])
        for n, (src, dst) in enumerate(zip(inputs, copies_in))
    ]
    for load in loads:
        load.start()
    for load in loads[:3]:
        load.wait()

    rows = pg_v.shape[0]
    zero4 = jnp.zeros((4, CZ), F32)
    w16s = jnp.concatenate([LOGIT * wt_ref[...].astype(F32), zero4], axis=0).astype(BF)
    zero32 = jnp.zeros((32, CZ), BF)

    def weights(i):
        gpad = jnp.concatenate([gpair_ref[:, i, :].astype(F32), zero4], axis=0).astype(BF)
        return jnp.concatenate([w16s, gpad], axis=0)

    stores = []
    parts = pg_sem.shape[0]
    step = rows // parts
    for b in range(rows // 4):
        for half in range(2):
            first, second = 4 * b + 2 * half, 4 * b + 2 * half + 1
            left = [zero32] * 4
            right = [zero32] * 4
            left[2 * half], right[2 * half + 1] = weights(first), weights(second)
            block = jnp.concatenate(
                [jnp.concatenate(left, axis=0), jnp.concatenate(right, axis=0)], axis=1
            )
            out = dot(turn_ref[b], block, 1, 0)
            pg_v[first] = out[:, :CZ].astype(BF)
            pg_v[second] = out[:, CZ:].astype(BF)
        if 4 * (b + 1) % step == 0:
            p = 4 * (b + 1) // step - 1
            store = pltpu.make_async_copy(
                pg_v.at[pl.ds(p * step, step)], outs[0].at[pl.ds(p * step, step)], pg_sem.at[p]
            )
            store.start()
            stores.append(store)

    for load in loads[3:]:
        load.wait()
    finish_body(sizes, *copies_in[3:], *results)
    for n, (src, dst) in enumerate(zip(results, outs[1:])):
        store = pltpu.make_async_copy(src, dst, out_sem.at[n])
        store.start()
        stores.append(store)
    for store in stores:
        store.wait()


def finish_body(
    sizes,
    kd_ref,
    kv_ref,
    query_ref,
    small_ref,
    hw_ref,
    qp_ref,
    kp_ref,
    vp_ref,
    rot_ref,
    trans_ref,
    gp_ref,
    qg_out,
    qpg_out,
    qfg_out,
    kg_out,
    vg_out,
    kpg_out,
    vpg_out,
    kfg_out,
    bw_out,
    hw_out,
):
    n0, n1, n2, m0, m1 = sizes
    share, qshare = kd_ref.shape[0], query_ref.shape[0]
    rows, cols = gp_ref.shape[1], kp_ref.shape[2]
    i0, i1, i2 = (lax.axis_index(a) for a in ROW)
    j0, j1 = (lax.axis_index(a) for a in COL)
    r = (i0 * n1 + i1) * n2 + i2
    c = j0 * m1 + j1

    def pick(count, width, at):
        return (iota((count, width), 1) == iota((count, width), 0) + at).astype(F32)

    def take(sel, array):
        return dot(sel, array, 1, 1, HIGHEST)

    def frames(start, count):
        base = pl.multiple_of((start // 128) * 128, 128)
        sel = pick(count, 128, start - base)
        rot = [take(sel, rot_ref[x, :, pl.ds(base, 128)]) for x in range(3)]
        return rot, take(sel, trans_ref[:, pl.ds(base, 128)])

    def column(a, y):
        return a[:, y : y + 1]

    def total(a):
        return jnp.sum(a, axis=1, keepdims=True)

    def put_frame(out, parts):
        count = parts[0][0].shape[0]
        for x in range(3):
            lane = iota((count, 128), 1)
            wide = jnp.zeros((count, 128), F32)
            for y in range(4):
                wide = jnp.where(lane == y, parts[x][y], wide)
            if count % 8:
                wide = jnp.concatenate([wide, jnp.zeros((8 - count % 8, 128), F32)], axis=0)
            out[x] = wide.T[0:4, :count]

    rot, anchor = frames(r * rows + c * qshare, qshare)
    local_sel = pick(qshare, rows, c * qshare)
    summed = query_ref[...]
    qg_out[...] = summed[:, 0:192]
    dqg = [summed[:, 192 + 48 * x : 240 + 48 * x] for x in range(3)]
    opt = [summed[:, 336 + 96 * x : 432 + 96 * x] for x in range(3)]
    local = [take(local_sel, qp_ref[y]) for y in range(3)]
    cotan = [gp_ref[y, pl.ds(c * qshare, qshare), :] for y in range(3)]
    for y in range(3):
        qpg_out[y] = sum(column(rot[x], y) * dqg[x] for x in range(3))
    parts = []
    for x in range(3):
        shifted = opt[x] - column(anchor, x)
        turned = sum(column(rot[x], y) * cotan[y] for y in range(3))
        parts.append(
            [total(dqg[x] * local[y]) + total(shifted * cotan[y]) for y in range(3)]
            + [total(dqg[x]) - total(turned)]
        )
    put_frame(qfg_out, parts)

    rot, anchor = frames(c * cols + r * share, share)
    local_sel = pick(share, cols, r * share)
    summed = kd_ref[...]
    kg_out[...] = summed[:, 0:192]
    dkg = [summed[:, 192 + 48 * x : 240 + 48 * x] for x in range(3)]
    summed = kv_ref[...]
    vg_out[...] = summed[:, 0:192]
    dvg = [summed[:, 192 + 96 * x : 288 + 96 * x] for x in range(3)]
    klocal = [take(local_sel, kp_ref[y]) for y in range(3)]
    vlocal = [take(local_sel, vp_ref[y]) for y in range(3)]
    for y in range(3):
        kpg_out[y] = sum(column(rot[x], y) * dkg[x] for x in range(3))
        vpg_out[y] = sum(column(rot[x], y) * dvg[x] for x in range(3))
    parts = []
    for x in range(3):
        parts.append(
            [total(dkg[x] * klocal[y]) + total(dvg[x] * vlocal[y]) for y in range(3)]
            + [total(dkg[x]) + total(dvg[x])]
        )
    put_frame(kfg_out, parts)

    bw_out[...] = small_ref[0:H, :]
    raw = hw_ref[...]
    hw_out[...] = small_ref[12:13, 0:H] * (-0.5 * LOGIT * POINT) / (1.0 + jnp.exp(-raw))


def per_device(
    sizes,
    pair_rep,
    bias_weight,
    head_weight,
    queries,
    key_vectors,
    values,
    query_points,
    key_points,
    value_points,
    rotations,
    translations,
    residue_count,
    grad_output,
    grad_points,
    grad_pair,
):
    n0, n1, n2, m0, m1 = sizes
    cols_n = m0 * m1
    rows, cols = pair_rep.shape[:2]
    share, qshare = cols // (n0 * n1 * n2), rows // cols_n
    head_row = head_weight.reshape(1, H)
    grad_points_t = jnp.transpose(grad_points, (0, 2, 1))
    hbm = pl.BlockSpec(memory_space=pl.ANY)
    dma = pltpu.SemaphoreType.DMA
    params = dict(vmem_limit_bytes=VMEM_BYTES)

    def buf(*shape, dtype=F32):
        return pltpu.VMEM(shape, dtype)

    def like(array):
        space = pltpu.VMEM if array.size > 1 else pltpu.SMEM
        return space(array.shape, array.dtype)

    weight_t = bias_weight.T
    grad_pair_t = jnp.transpose(grad_pair, (1, 0, 2))
    operands = (
        weight_t,
        head_row,
        queries.T,
        key_vectors,
        values,
        query_points,
        key_points,
        value_points,
        rotations,
        translations,
        residue_count,
        grad_output.T,
        grad_points_t,
        grad_pair_t,
    )
    sums = (
        jax.ShapeDtypeStruct((rows // 4, cols, 128), BF),
        jax.ShapeDtypeStruct((share, KD), F32),
        jax.ShapeDtypeStruct((share, KV), F32),
        jax.ShapeDtypeStruct((qshare, QF), F32),
        jax.ShapeDtypeStruct((16, CZ), F32),
    )

    def staged(width):
        return (
            buf(width, cols),
            buf(n0 * n1, n2, share, width),
            buf(n0 * n1, share, width),
            buf(n0, n1, share, width),
            buf(n1 - 1, n0, share, width),
            buf(n0, share, width),
            buf(n0 - 1, share, width),
        )

    def pairs(*counts):
        return tuple(dma((n,)) for n in counts for _ in range(2))

    levels = (m1 * n0, m0 * n2, n1)
    turned, kd_sum, kv_sum, query_sum, small_sum = pl.pallas_call(
        functools.partial(tile_kernel, sizes),
        name="tile",
        out_shape=sums,
        in_specs=[hbm] * (1 + len(operands)),
        out_specs=(hbm,) * 5,
        scratch_shapes=[
            *[like(a) for a in operands],
            like(pair_rep),
            *[like(a) for a in sums],
            buf(cols // 128, rows * 32, 128),
            buf(H * rows, cols),
            buf(H * rows, cols),
            buf(H * rows, cols),
            buf(H * 32, rows),
            buf(H * 32, cols),
            buf(H * 48, rows),
            buf(H * 48, cols),
            buf(H * rows, 128),
            buf(8, 128),
            buf(16, 128),
            buf(cols_n - 1, 16, 128),
            buf(H * 32, 3 * rows, dtype=BF),
            buf(H * 48, 3 * rows, dtype=BF),
            buf(H * 32, rows),
            buf(H * 32, rows),
            buf(H * 24, rows),
            buf(QF, rows),
            buf(cols_n, qshare, QF),
            buf(m0 - 1, m1, qshare, QF),
            buf(m1, qshare, QF),
            buf(max(m1 - 1, 1), qshare, QF),
            staged(KD),
            staged(KV),
            tuple(b for n in levels for b in (buf(16, CZ), buf(n - 1, 16, CZ))),
            dma((len(operands),)),
            dma((4,)),
            dma((len(sums),)),
            pairs(cols_n - 1),
            pairs(m0 - 1),
            pairs(max(m1 - 1, 1)),
            pairs(1, n1 - 1, n0 - 1),
            pairs(1, n1 - 1, n0 - 1),
            pairs(*[n - 1 for n in levels]),
        ],
        compiler_params=pltpu.CompilerParams(collective_id=0, has_side_effects=True, **params),
    )(pair_rep, *operands)
    operands = (
        turned,
        weight_t,
        grad_pair_t,
        kd_sum,
        kv_sum,
        query_sum,
        small_sum,
        head_row,
        query_points,
        key_points,
        value_points,
        rotations,
        translations,
        grad_points_t,
    )
    results = (
        jax.ShapeDtypeStruct((qshare, 192), F32),
        jax.ShapeDtypeStruct((3, qshare, 48), F32),
        jax.ShapeDtypeStruct((3, 4, qshare), F32),
        jax.ShapeDtypeStruct((share, 192), F32),
        jax.ShapeDtypeStruct((share, 192), F32),
        jax.ShapeDtypeStruct((3, share, 48), F32),
        jax.ShapeDtypeStruct((3, share, 96), F32),
        jax.ShapeDtypeStruct((3, 4, share), F32),
        jax.ShapeDtypeStruct((H, CZ), F32),
        jax.ShapeDtypeStruct((1, H), F32),
    )
    pair_grad, qg, qpg, qfg, kg, vg, kpg, vpg, kfg, bw, hw = pl.pallas_call(
        functools.partial(finish_kernel, sizes),
        name="finish",
        out_shape=(jax.ShapeDtypeStruct(pair_rep.shape, BF), *results),
        in_specs=[hbm] * len(operands),
        out_specs=(hbm,) * 11,
        scratch_shapes=[
            *[like(a) for a in operands],
            *[like(a) for a in results],
            like(pair_rep),
            dma((len(operands),)),
            dma((4,)),
            dma((len(results),)),
        ],
        compiler_params=pltpu.CompilerParams(**params),
    )(*operands)

    def swap(a):
        return jnp.transpose(a, (0, 2, 1))

    return (
        pair_grad,
        qg.T,
        swap(qpg),
        qfg,
        kg.T,
        vg.T,
        swap(kpg),
        swap(vpg),
        kfg,
        bw.T,
        hw.reshape(H),
    )


def solution(mesh, sizes=(4, 4, 2, 4, 2)):
    finer = Mesh(mesh.devices.reshape(sizes), ROW_COL)
    in_specs = (
        P(ROW, COL, None),
        P(),
        P(),
        P(None, ROW),
        P(None, COL),
        P(None, COL),
        P(None, None, ROW),
        P(None, None, COL),
        P(None, None, COL),
        P(),
        P(),
        P(),
        P(None, ROW),
        P(None, None, ROW),
        P(ROW, None, None),
    )
    out_specs = (
        P(ROW, COL, None),
        P(None, ROW_COL),
        P(None, None, ROW_COL),
        P(None, None, ROW_COL),
        P(None, COL_ROW),
        P(None, COL_ROW),
        P(None, None, COL_ROW),
        P(None, None, COL_ROW),
        P(None, None, COL_ROW),
        P(),
        P(),
    )
    return jax.shard_map(
        functools.partial(per_device, sizes),
        mesh=finer,
        in_specs=in_specs,
        out_specs=out_specs,
        check_vma=False,
    )
```

time: 66.1 us -> 40.6 us (0.61)
  local copies, waits for them, and re-layouts: 19.5 us -> 0 us
  Pallas kernels: 44.6 us -> 39.2 us
    unnamed x35 -> x0, local copies, waits for them, and re-layouts: 19.5 us -> none
    pallas_call x1, Pallas kernels: 41.5 us -> 34.5 us  [per_device(): pl.pallas_call(functools.partial(tile_kernel, sizes), name='tile', out_sh...]
    pallas_call x1, Pallas kernels: 3.06 us -> 4.7 us  [per_device(): pl.pallas_call(functools.partial(finish_kernel, sizes), name='finish', ou...]
where the time goes in v2:
time: 40.6 us; the launch traced here: 40.5 us
  Pallas kernels  39.2 us (97%)
  between operations  1.3 us (3%)
    pallas_call x1, Pallas kernels, per_device(): pl.pallas_call(functools.partial(tile_kernel, sizes), name='tile', out_sh...  34.5 us
    pallas_call x1, Pallas kernels, per_device(): pl.pallas_call(functools.partial(finish_kernel, sizes), name='finish', ou...  4.7 us

profile of v2, /device:TPU:1, one launch (start us, length us, event | category | flops | bytes accessed | tf_op | source)
XLA Modules:
  0.0 40.5 jit_solution(10828473410925545400)
XLA Ops:
  1.3 34.5 %tile.1 = (bf16[16,256,128]{2,1,0:T(8,128)(2,1)}, f32[8,384]{1,0:T(8,128)}, f32[8,512]{1,0:T(8,128)}, f32[8,640]{1,0:T(8,128)}, f32[16,128]{1,0:T(8,128)}) custom-call(bf16[64,256,128]{2,1,0:T(8,128)(2,1)} %pair_hbm.1, bf16[12,128]{1,0:T(8,128)(2,1)} %bitcast.20, f32[1,12]{1,0:T(1,128)} %bitcast.22, f32[64,192]{1,0:T(8,128)} %bitcast.18, ...), custom_call_target="tpu_custom_call" | custom-call | tf_op jit(solution)/shard_map/tile/pallas_call | solution.py:810
  35.8 4.7 %finish.1 = (bf16[64,256,128]{2,1,0:T(8,128)(2,1)}, f32[8,192]{1,0:T(8,128)}, f32[3,8,48]{2,1,0:T(8,128)}, f32[3,4,8]{2,1,0:T(4,128)}, f32[8,192]{1,0:T(8,128)},...) custom-call(bf16[16,256,128]{2,1,0:T(8,128)(2,1)} %get-tuple-element, ...), custom_call_target="tpu_custom_call" | custom-call | tf_op jit(solution)/shard_map/finish/pallas_call | solution.py:885

commit v3 on v2

--- a/solution.py
+++ b/solution.py
@@ -16,6 +16,14 @@
 
 H, C, PQ, PV, CZ = 12, 16, 4, 8, 128
 KD, KV, QF = 384, 512, 640
+ROT_Q, ROT_K, SEL_Q, SEL_D, SEL_V, SEL_C = 0, 9, 18, 30, 36, 45
+
+
+def frame_lines(values, count):
+    diagonal = iota((count, 128), 0) == iota((count, 128), 1)
+    return [
+        jnp.sum(jnp.where(diagonal, v, 0.0), axis=0, keepdims=True)[:, :count] for v in values
+    ]
 LOGIT = math.sqrt(1.0 / 3.0)
 POINT = math.sqrt(2.0 / (9.0 * PQ))
 INNER = 1.0 / math.sqrt(C)
@@ -79,7 +87,7 @@
     *refs,
 ):
     inputs, refs = refs[:14], refs[14:]
-    sums, refs = refs[:5], refs[5:]
+    sums, refs = refs[:6], refs[6:]
     copies_in, refs = refs[:14], refs[14:]
     tile_body(sizes, pair_hbm, inputs, copies_in, *sums, *copies_in, *refs)
 
@@ -94,6 +102,7 @@
     kv_hbm,
     query_hbm,
     small_hbm,
+    sel_hbm,
     wt_ref,
     hw_ref,
     q_ref,
@@ -114,7 +123,14 @@
     kv_out,
     query_out,
     small_out,
+    sel_out,
+    turn_buf,
+    wide_d,
+    wide_v,
     s_ref,
+    pair_t,
+    ub_ref,
+    x_ref,
     e_ref,
     p_ref,
     d_ref,
@@ -124,6 +140,7 @@
     v48,
     vec,
     own_peak,
+    own_dist,
     stat_own,
     stat_in,
     q_pack,
@@ -196,7 +213,7 @@
         pltpu.make_async_copy(src, dst, in_sem.at[n])
         for n, (src, dst) in enumerate(zip(inputs, copies_in))
     ]
-    for load in smalls:
+    for load in smalls + loads[:2]:
         load.start()
 
     barrier = pltpu.get_barrier_semaphore()
@@ -211,7 +228,7 @@
             )
             expected += 1
 
-    for load in loads:
+    for load in loads[2:]:
         load.start()
     for load in smalls:
         load.wait()
@@ -270,20 +287,6 @@
             [jnp.ones((1, cols), F32), jnp.sum(kh * kh, axis=0, keepdims=True), zero_k], axis=0
         )
 
-    def pair_row(at):
-        return jnp.concatenate(
-            [s_ref[a, pl.ds(at, rows, stride=32), :] for a in range(cols // 128)], axis=1
-        )
-
-    def put_pair_row(at, value):
-        for a in range(cols // 128):
-            s_ref[a, pl.ds(at, rows, stride=32), :] = value[:, 128 * a : 128 * a + 128]
-
-    def pair_block(at, count):
-        return jnp.concatenate(
-            [s_ref[a, at : at + count, :] for a in range(cols // 128)], axis=1
-        )
-
     w16 = jnp.concatenate([wt_ref[...].astype(F32), jnp.zeros((4, CZ), F32)], axis=0)
     w16b = w16.astype(BF)
 
@@ -293,46 +296,51 @@
         ).astype(BF)
         return gpad
 
+    e_ref[H:16] = jnp.zeros((16 - H, rows, cols), F32)
+    p_ref[H:16] = jnp.zeros((16 - H, rows, cols), F32)
     point_row = iota((16, 1), 0) < 12
     for h in range(H):
-        own = slice(h * rows, (h + 1) * rows)
         kb = k32[32 * h + 16 : 32 * h + 32, :]
         inner = dot6(q32[32 * h : 32 * h + 16, :], k32[32 * h : 32 * h + 16, :])
         dist = dot6(q32[32 * h + 16 : 32 * h + 32, :], jnp.where(point_row, -2.0 * kb, kb))
-        d_ref[own, :] = dist
-        e_ref[own, :] = inner - coef[:, h : h + 1] * dist
-        p_ref[own, :] = dot(
+        d_ref[h] = dist
+        e_ref[h] = inner - coef[:, h : h + 1] * dist
+        p_ref[h] = dot(
             three(g48[48 * h : 48 * h + 48, :], 0), three_rhs(v48[48 * h : 48 * h + 48, :]), 0, 0
         )
 
     for b in range(parts):
         loads[b].wait()
-        for ii in range(step):
-            i = b * step + ii
-            both = jnp.concatenate([w16b, stack(i)], axis=0)
-            proj = dot(both, pair_v[i], 1, 1)
-            for a in range(cols // 128):
-                s_ref[a, 32 * i : 32 * i + 32, :] = proj[:, 128 * a : 128 * a + 128]
+        for ib in range(b * step // 8, (b + 1) * step // 8):
+            proj = []
+            for i in range(8 * ib, 8 * ib + 8):
+                both = jnp.concatenate([w16b, stack(i)], axis=0)
+                if i % 4 == 3:
+                    proj.append(dot(both, pair_v[i], 1, 1))
+                else:
+                    pair_t[i] = pair_v[i].T
+                    proj.append(dot(both, pair_t[i], 1, 0))
+            s_ref[:, 8 * ib : 8 * ib + 8, :] = jnp.transpose(jnp.stack(proj), (1, 0, 2))
 
     valid = col_start + iota((1, cols), 1) < count_ref[0]
     lane = iota((rows, 128), 1)
     for h in range(H):
-        own = slice(h * rows, (h + 1) * rows)
-        prod = p_ref[own, :] + pair_row(16 + h)
-        logits = e_ref[own, :] + LOGIT * pair_row(h)
+        prod = p_ref[h] + s_ref[16 + h]
+        logits = e_ref[h] + LOGIT * s_ref[h]
         logits = jnp.where(valid, logits, -1000000000.0)
         peak = jnp.max(logits, axis=1, keepdims=True)
         e = jnp.exp(logits - peak)
         total = jnp.sum(e, axis=1, keepdims=True)
         upper = jnp.sum(e * prod, axis=1, keepdims=True)
-        e_ref[own, :] = e
-        p_ref[own, :] = prod
+        e_ref[h] = e
+        p_ref[h] = prod
         vec[h * rows : (h + 1) * rows, :] = jnp.where(
             lane == 0, peak + jnp.log(total), jnp.where(lane == 1, upper / total, peak)
         )
     blocks = H * rows // 128
     stat_own[...] = jnp.zeros_like(stat_own)
     own_peak[...] = jnp.zeros_like(own_peak)
+    own_dist[...] = jnp.zeros_like(own_dist)
     for b in range(blocks):
         turned = vec[128 * b : 128 * b + 128, :].T
         stat_own[b : b + 1, :] = turned[0:1]
@@ -345,15 +353,34 @@
         send(stat_own, stat_in.at[d - 1], stat_sems, d - 1, col_peer(d)) for d in range(1, cols_n)
     ]
 
+    for a in (6, 14, 22, 30):
+        s_ref[a : a + 2] = jnp.zeros((2, rows, cols), F32)
     for h in range(H):
         own = slice(h * rows, (h + 1) * rows)
-        e = e_ref[own, :]
+        e = e_ref[h]
         es = split(e)
+        ep = e * (p_ref[h] - vec[own, 1:2])
         ks = split(k32[32 * h : 32 * h + 32, :])
-        qa[32 * h : 32 * h + 32, :] = dot3(ks, split(e * (p_ref[own, :] - vec[own, 1:2])), 1, 1)
+        qa[32 * h : 32 * h + 32, :] = dot3(ks, split(ep), 1, 1)
         qb[32 * h : 32 * h + 32, :] = dot3(ks, es, 1, 1)
         qv[24 * h : 24 * h + 24, :] = dot3(split(v48[48 * h : 48 * h + 48, :]), es, 1, 1)[16:40]
-
+        s_ref[8 * (h % 2) + h // 2] = ep
+        s_ref[16 + 8 * (h % 2) + h // 2] = e
+        dist = d_ref[h]
+        vec[own, :] = jnp.where(
+            lane == 0,
+            jnp.sum(ep * dist, axis=1, keepdims=True),
+            jnp.sum(e * dist, axis=1, keepdims=True),
+        )
+    for b in range(blocks):
+        turned = vec[128 * b : 128 * b + 128, :].T
+        own_dist[b : b + 1, :] = turned[0:1]
+        own_dist[8 + b : 9 + b, :] = turned[1:2]
+    for ib in range(rows // 8):
+        by_query = jnp.transpose(s_ref[:, 8 * ib : 8 * ib + 8, :], (1, 0, 2))
+        for ii in range(8):
+            both = dot(jnp.concatenate(split(by_query[ii]), axis=0), pair_v[8 * ib + ii], 1, 0)
+            ub_ref[8 * ib + ii] = both[0:32] + both[32:64]
     for h in range(H):
         q_pack[32 * h : 32 * h + 32, :] = three(q32[32 * h : 32 * h + 32, :], 1)
         g_pack[48 * h : 48 * h + 48, :] = three(g48[48 * h : 48 * h + 48, :], 1)
@@ -369,103 +396,6 @@
     scale = jnp.exp(own_peak[...] - peak) / total
     shift = delta - stats[0][8:16]
     scale_t, delta_t = scale.T, delta.T
-
-    kind = iota((32, 1), 0)
-    is_vec = kind < 16
-
-    class Staged:
-        def __init__(self, refs, sems, out):
-            self.feat, self.kt, self.k1, self.p1, self.k2, self.p2, self.k3 = refs
-            self.sems = (sems[0:2], sems[2:4], sems[4:6])
-            self.out = out
-
-        def turn(self):
-            share = self.kt.shape[2]
-            per = 128 // (share * n2)
-            for a in range(self.feat.shape[0] // 128):
-                for b in range(cols // 128):
-                    block = self.feat[128 * a : 128 * a + 128, 128 * b : 128 * b + 128].T
-                    self.kt[b * per : (b + 1) * per, :, :, 128 * a : 128 * a + 128] = block.reshape(
-                        per, n2, share, 128
-                    )
-
-        def send1(self):
-            other = lax.rem(i2 + 1, n2)
-            self.copies = [send(self.kt.at[:, other], self.k1, self.sems[0], 0, {"row_2": other})]
-
-        def wait(self):
-            for copy in self.copies:
-                copy.wait()
-
-        def send2(self):
-            self.wait()
-            self.p1[...] = (self.kt[:, i2] + self.k1[...]).reshape(self.p1.shape)
-            self.copies = []
-            for d in range(1, n1):
-                to = lax.rem(i1 + d, n1)
-                self.copies.append(
-                    send(self.p1.at[:, to], self.k2.at[d - 1], self.sems[1], d - 1, {"row_1": to})
-                )
-
-        def send3(self):
-            self.wait()
-            self.p2[...] = self.p1[:, i1] + functools.reduce(
-                jnp.add, [self.k2[d] for d in range(n1 - 1)]
-            )
-            self.copies = []
-            for d in range(1, n0):
-                to = lax.rem(i0 + d, n0)
-                self.copies.append(
-                    send(self.p2.at[to], self.k3.at[d - 1], self.sems[2], d - 1, {"row_0": to})
-                )
-
-        def finish(self):
-            self.wait()
-            self.out[...] = self.p2[i0] + functools.reduce(
-                jnp.add, [self.k3[d] for d in range(n0 - 1)]
-            )
-
-    side_d = Staged(kd_refs, kd_sems, kd_out)
-    side_v = Staged(kv_refs, kv_sems, kv_out)
-
-    head_sum = jnp.zeros((1, 128), F32)
-    lane1 = iota((1, 128), 1)
-    side_d.feat[336:KD, :] = jnp.zeros((KD - 336, cols), F32)
-    side_v.feat[480:KV, :] = jnp.zeros((KV - 480, cols), F32)
-    for h in range(H):
-        own = slice(h * rows, (h + 1) * rows)
-        at = (slice(rows * (h % 2), rows * (h % 2) + rows), slice(h // 2, h // 2 + 1))
-        attn = e_ref[own, :] * scale_t[at]
-        dlog = attn * (p_ref[own, :] - delta_t[at])
-        moment = jnp.sum(jnp.sum(dlog * d_ref[own, :], axis=0, keepdims=True), axis=1, keepdims=True)
-        head_sum = jnp.where(lane1 == h, moment, head_sum)
-        put_pair_row(h, dlog)
-        put_pair_row(16 + h, attn)
-        e_ref[own, :] = attn
-        two = 2.0 * coef[:, h : h + 1]
-        kd = dot(q_pack[32 * h : 32 * h + 32, :], three_rhs(dlog), 1, 0)
-        col_sum = kd[29:30]
-        kd = jnp.where(is_vec, kd, two * (kd - k32[32 * h : 32 * h + 32, :] * col_sum))
-        side_d.feat[16 * h : 16 * h + 16, :] = kd[0:16]
-        for x in range(3):
-            to = 192 + 48 * x + 4 * h
-            side_d.feat[to : to + 4, :] = kd[16 + 4 * x : 20 + 4 * x]
-    side_d.turn()
-    side_d.send1()
-
-    for h in range(H):
-        own = slice(h * rows, (h + 1) * rows)
-        ka = dot(g_pack[48 * h : 48 * h + 48, :], three_rhs(e_ref[own, :]), 1, 0)
-        side_v.feat[16 * h : 16 * h + 16, :] = ka[0:16]
-        for x in range(3):
-            to = 192 + 96 * x + 8 * h
-            side_v.feat[to : to + 8, :] = ka[16 + 8 * x : 24 + 8 * x]
-    side_v.turn()
-    side_v.send1()
-
-    acc = jnp.zeros((16, CZ), F32)
-    for i in range(rows):
-        acc = acc + dot(pair_block(32 * i, 16).astype(BF), pair_v[i], 1, 0)
 
     class Small:
         def __init__(self, value):
@@ -497,8 +427,110 @@
                 w_refs[2 * self.level][...] = total
             return total
 
-    small = Small(jnp.where(iota((16, 1), 0) == 12, head_sum, LOGIT * acc))
+    half = rows
+    scale_h = jnp.concatenate([scale[:, :half], scale[:, half:]], axis=0)
+    shift_h = jnp.concatenate([shift[:, :half], shift[:, half:]], axis=0)
+    acc = jnp.zeros((16, CZ), F32)
+    for i in range(rows):
+        acc = acc + scale_h[:, i : i + 1] * (
+            ub_ref[i, 0:16] - shift_h[:, i : i + 1] * ub_ref[i, 16:32]
+        )
+    moment = scale * (own_dist[0:8, :] - shift * own_dist[8:16, :])
+    lane8, row8 = iota((8, 128), 1), iota((8, 128), 0)
+    even = jnp.sum(jnp.where(lane8 < half, moment, 0.0), axis=1, keepdims=True)
+    odd = jnp.sum(jnp.where(lane8 < half, 0.0, moment), axis=1, keepdims=True)
+    spread = jnp.where(lane8 == 2 * row8, even, jnp.where(lane8 == 2 * row8 + 1, odd, 0.0))
+    head_sum = jnp.sum(spread, axis=0, keepdims=True)
+    small = Small(jnp.where(iota((16, 1), 0) == 6, head_sum, LOGIT * acc))
     small.send("z")
+
+    kind = iota((32, 1), 0)
+    is_vec = kind < 16
+
+    class Staged:
+        def __init__(self, refs, sems, out):
+            self.feat, self.kt, self.k1, self.p1, self.k2, self.p2, self.k3 = refs
+            self.sems = (sems[0:2], sems[2:4], sems[4:6])
+            self.out = out
+
+        def turn(self):
+            share = self.kt.shape[2]
+            per = 128 // (share * n2)
+            for a in range(self.feat.shape[0] // 128):
+                for b in range(cols // 128):
+                    block = self.feat[128 * a : 128 * a + 128, 128 * b : 128 * b + 128].T
+                    self.kt[b * per : (b + 1) * per, :, :, 128 * a : 128 * a + 128] = block.reshape(
+                        per, n2, share, 128
+                    )
+
+        def send1(self):
+            other = lax.rem(i2 + 1, n2)
+            self.copies = [send(self.kt.at[:, other], self.k1, self.sems[0], 0, {"row_2": other})]
+
+        def wait(self):
+            for copy in self.copies:
+                copy.wait()
+
+        def send2(self):
+            self.wait()
+            self.p1[...] = (self.kt[:, i2] + self.k1[...]).reshape(self.p1.shape)
+            self.copies = []
+            for d in range(1, n1):
+                to = lax.rem(i1 + d, n1)
+                self.copies.append(
+                    send(self.p1.at[:, to], self.k2.at[d - 1], self.sems[1], d - 1, {"row_1": to})
+                )
+
+        def send3(self):
+            self.wait()
+            self.p2[...] = self.p1[:, i1] + functools.reduce(
+                jnp.add, [self.k2[d] for d in range(n1 - 1)]
+            )
+            self.copies = []
+            for d in range(1, n0):
+                to = lax.rem(i0 + d, n0)
+                self.copies.append(
+                    send(self.p2.at[to], self.k3.at[d - 1], self.sems[2], d - 1, {"row_0": to})
+                )
+
+        def finish(self):
+            self.wait()
+            self.out[...] = self.p2[i0] + functools.reduce(
+                jnp.add, [self.k3[d] for d in range(n0 - 1)]
+            )
+
+    side_d = Staged(kd_refs, kd_sems, kd_out)
+    side_v = Staged(kv_refs, kv_sems, kv_out)
+
+    side_d.feat[336:KD, :] = jnp.zeros((KD - 336, cols), F32)
+    side_v.feat[480:KV, :] = jnp.zeros((KV - 480, cols), F32)
+    for h in range(H):
+        own = slice(h * rows, (h + 1) * rows)
+        at = (slice(rows * (h % 2), rows * (h % 2) + rows), slice(h // 2, h // 2 + 1))
+        attn = e_ref[h] * scale_t[at]
+        dlog = attn * (p_ref[h] - delta_t[at])
+        p_ref[h] = dlog
+        e_ref[h] = attn
+        two = 2.0 * coef[:, h : h + 1]
+        kd = dot(q_pack[32 * h : 32 * h + 32, :], three_rhs(dlog), 1, 0)
+        col_sum = kd[29:30]
+        kd = jnp.where(is_vec, kd, two * (kd - k32[32 * h : 32 * h + 32, :] * col_sum))
+        side_d.feat[16 * h : 16 * h + 16, :] = kd[0:16]
+        for x in range(3):
+            to = 192 + 48 * x + 4 * h
+            side_d.feat[to : to + 4, :] = kd[16 + 4 * x : 20 + 4 * x]
+    side_d.turn()
+    side_d.send1()
+
+    for h in range(H):
+        own = slice(h * rows, (h + 1) * rows)
+        ka = dot(g_pack[48 * h : 48 * h + 48, :], three_rhs(e_ref[h]), 1, 0)
+        side_v.feat[16 * h : 16 * h + 16, :] = ka[0:16]
+        for x in range(3):
+            to = 192 + 96 * x + 8 * h
+            side_v.feat[to : to + 8, :] = ka[16 + 8 * x : 24 + 8 * x]
+    side_v.turn()
+    side_v.send1()
 
     side_d.send2()
 
@@ -530,10 +562,70 @@
 
     side_v.send2()
 
+    for ib in range(rows // 8):
+        some = slice(8 * ib, 8 * ib + 8)
+        x_ref[some, 0:16, :] = jnp.transpose(p_ref[:, some, :], (1, 0, 2)).astype(BF)
+        x_ref[some, 16:32, :] = jnp.transpose(e_ref[:, some, :], (1, 0, 2)).astype(BF)
     for b in range(rows // 4):
-        turn_v[b] = pair_block(128 * b, 128).T.astype(BF)
+        turn_v[b] = x_ref[4 * b : 4 * b + 4].reshape(128, cols).T
     turn_copy = pltpu.make_async_copy(turn_v, turn_hbm, out_sem.at[0])
     turn_copy.start()
+
+    share = kd_out.shape[0]
+
+    def frames(start):
+        base = pl.multiple_of((start // 128) * 128, 128)
+        sel = iota((share, 128), 1) == iota((share, 128), 0) + (start - base)
+
+        def every_lane(row):
+            one = jnp.sum(jnp.where(sel, row, 0.0), axis=1, keepdims=True)
+            return jnp.broadcast_to(one, (share, 128))
+
+        rot = [
+            [every_lane(rot_ref[x, pl.ds(y, 1), pl.ds(base, 128)]) for y in range(3)]
+            for x in range(3)
+        ]
+        return rot, [every_lane(trans_ref[pl.ds(x, 1), pl.ds(base, 128)]) for x in range(3)]
+
+    rot, anchor = frames(r * rows + c * share)
+    key_rot, _ = frames(c * cols + r * share)
+    key_base = pl.multiple_of((r * share // 128) * 128, 128)
+    key_at = pl.multiple_of(lax.rem(r * share, 128), 8)
+    query_at = pl.multiple_of(c * share, 8)
+
+    def hand_over(to, blocks, wide, at):
+        for begin, block in blocks:
+            wide[begin : begin + block.shape[0], :] = block
+        for n in range(1, wide.shape[0] // 128):
+            turn_buf[0 : wide.shape[1], :] = wide[128 * n : 128 * n + 128, :].T
+            sel_out[to + n - 1] = turn_buf[pl.ds(at, share), :]
+
+    constants = []
+    for x in range(3):
+        for y in range(3):
+            sel_out[ROT_Q + 3 * x + y] = rot[x][y]
+            sel_out[ROT_K + 3 * x + y] = key_rot[x][y]
+    cotan = [gp_ref[y, pl.ds(query_at, share), :] for y in range(3)]
+    sums = [jnp.sum(a, axis=1, keepdims=True) for a in cotan]
+    for x in range(3):
+        constants += [-anchor[x][:, 0:1] * sums[y] for y in range(3)]
+        constants.append(-sum(rot[x][y][:, 0:1] * sums[y] for y in range(3)))
+    for n, line in enumerate(frame_lines(constants, share)):
+        sel_out[SEL_C + n // share, n % share : n % share + 1, 0:share] = line
+    qfeat[...] = jnp.zeros_like(qfeat)
+    wide_d[...] = jnp.zeros_like(wide_d)
+    wide_v[...] = jnp.zeros_like(wide_v)
+    for y in range(3):
+        local, cotan_y = qp_ref[y], gp_ref[y].T
+        blocks = [(192 + 48 * x, local) for x in range(3)]
+        blocks += [(336 + 96 * x, cotan_y) for x in range(3)]
+        hand_over(SEL_Q + 4 * y, blocks, qfeat, query_at)
+        local = kp_ref[y, :, pl.ds(key_base, 128)]
+        hand_over(SEL_D + 2 * y, [(192 + 48 * x, local) for x in range(3)], wide_d, key_at)
+        local = vp_ref[y, :, pl.ds(key_base, 128)]
+        hand_over(SEL_V + 3 * y, [(192 + 96 * x, local) for x in range(3)], wide_v, key_at)
+    sel_copy = pltpu.make_async_copy(sel_out, sel_hbm, out_sem.at[5])
+    sel_copy.start()
 
     small.add()
     small.send("x")
@@ -562,22 +654,30 @@
     ]
     for copy in outs:
         copy.start()
-    for copy in outs + [turn_copy]:
+    for copy in outs + [turn_copy, sel_copy]:
         copy.wait()
 
 
-def finish_kernel(sizes, *refs):
-    inputs, refs = refs[:14], refs[14:]
+def finish_kernel(*refs):
+    inputs, refs = refs[:9], refs[9:]
     outs, refs = refs[:11], refs[11:]
-    copies_in, refs = refs[:14], refs[14:]
+    copies_in, refs = refs[:9], refs[9:]
     results, (pg_v, in_sem, pg_sem, out_sem) = refs[:10], refs[10:]
     turn_ref, wt_ref, gpair_ref = copies_in[:3]
     loads = [
         pltpu.make_async_copy(src, dst, in_sem.at[n])
         for n, (src, dst) in enumerate(zip(inputs, copies_in))
     ]
-    for load in loads:
+    for load in loads[3:] + loads[:3]:
         load.start()
+    for load in loads[3:]:
+        load.wait()
+    finish_body(*copies_in[3:], *results)
+    stores = []
+    for n, (src, dst) in enumerate(zip(results, outs[1:])):
+        store = pltpu.make_async_copy(src, dst, out_sem.at[n])
+        store.start()
+        stores.append(store)
     for load in loads[:3]:
         load.wait()
 
@@ -590,7 +690,6 @@
         gpad = jnp.concatenate([gpair_ref[:, i, :].astype(F32), zero4], axis=0).astype(BF)
         return jnp.concatenate([w16s, gpad], axis=0)
 
-    stores = []
     parts = pg_sem.shape[0]
     step = rows // parts
     for b in range(rows // 4):
@@ -613,30 +712,17 @@
             store.start()
             stores.append(store)
 
-    for load in loads[3:]:
-        load.wait()
-    finish_body(sizes, *copies_in[3:], *results)
-    for n, (src, dst) in enumerate(zip(results, outs[1:])):
-        store = pltpu.make_async_copy(src, dst, out_sem.at[n])
-        store.start()
-        stores.append(store)
     for store in stores:
         store.wait()
 
 
 def finish_body(
-    sizes,
     kd_ref,
     kv_ref,
     query_ref,
     small_ref,
+    sel_ref,
     hw_ref,
-    qp_ref,
-    kp_ref,
-    vp_ref,
-    rot_ref,
-    trans_ref,
-    gp_ref,
     qg_out,
     qpg_out,
     qfg_out,
@@ -648,87 +734,70 @@
     bw_out,
     hw_out,
 ):
-    n0, n1, n2, m0, m1 = sizes
-    share, qshare = kd_ref.shape[0], query_ref.shape[0]
-    rows, cols = gp_ref.shape[1], kp_ref.shape[2]
-    i0, i1, i2 = (lax.axis_index(a) for a in ROW)
-    j0, j1 = (lax.axis_index(a) for a in COL)
-    r = (i0 * n1 + i1) * n2 + i2
-    c = j0 * m1 + j1
-
-    def pick(count, width, at):
-        return (iota((count, width), 1) == iota((count, width), 0) + at).astype(F32)
-
-    def take(sel, array):
-        return dot(sel, array, 1, 1, HIGHEST)
-
-    def frames(start, count):
-        base = pl.multiple_of((start // 128) * 128, 128)
-        sel = pick(count, 128, start - base)
-        rot = [take(sel, rot_ref[x, :, pl.ds(base, 128)]) for x in range(3)]
-        return rot, take(sel, trans_ref[:, pl.ds(base, 128)])
-
-    def column(a, y):
-        return a[:, y : y + 1]
-
-    def total(a):
-        return jnp.sum(a, axis=1, keepdims=True)
-
-    def put_frame(out, parts):
-        count = parts[0][0].shape[0]
-        for x in range(3):
-            lane = iota((count, 128), 1)
-            wide = jnp.zeros((count, 128), F32)
-            for y in range(4):
-                wide = jnp.where(lane == y, parts[x][y], wide)
-            if count % 8:
-                wide = jnp.concatenate([wide, jnp.zeros((8 - count % 8, 128), F32)], axis=0)
-            out[x] = wide.T[0:4, :count]
-
-    rot, anchor = frames(r * rows + c * qshare, qshare)
-    local_sel = pick(qshare, rows, c * qshare)
-    summed = query_ref[...]
-    qg_out[...] = summed[:, 0:192]
-    dqg = [summed[:, 192 + 48 * x : 240 + 48 * x] for x in range(3)]
-    opt = [summed[:, 336 + 96 * x : 432 + 96 * x] for x in range(3)]
-    local = [take(local_sel, qp_ref[y]) for y in range(3)]
-    cotan = [gp_ref[y, pl.ds(c * qshare, qshare), :] for y in range(3)]
-    for y in range(3):
-        qpg_out[y] = sum(column(rot[x], y) * dqg[x] for x in range(3))
-    parts = []
+    share = kd_ref.shape[0]
+
+    def lanes(width, x, *segments):
+        lane = iota((share, width), 1) + 128
+        return functools.reduce(
+            jnp.logical_or,
+            [(lane >= b + w * x) & (lane < b + w * x + w) for b, w in segments],
+        )
+
+    def segment_sum(values, mask):
+        kept = jnp.where(mask, values, 0.0)
+        parts = [kept[:, 128 * n : 128 * n + 128] for n in range(kept.shape[1] // 128)]
+        return functools.reduce(jnp.add, parts)
+
+    def handed(at, count):
+        return jnp.concatenate([sel_ref[at + n] for n in range(count)], axis=1)
+
+    def put(out, lines):
+        for n, line in enumerate(lines):
+            out[n // 4, n % 4 : n % 4 + 1, :] = line
+
+    query, key_d, key_v = query_ref[...], kd_ref[...], kv_ref[...]
+    qg_out[...] = query[:, 0:192]
+    kg_out[...] = key_d[:, 0:192]
+    vg_out[...] = key_v[:, 0:192]
+    turned = [
+        (qpg_out, ROT_Q, [query[:, 192 + 48 * x : 240 + 48 * x] for x in range(3)]),
+        (kpg_out, ROT_K, [key_d[:, 192 + 48 * x : 240 + 48 * x] for x in range(3)]),
+        (vpg_out, ROT_K, [key_v[:, 192 + 96 * x : 288 + 96 * x] for x in range(3)]),
+    ]
+
+    query, key_d, key_v = query[:, 128:], key_d[:, 128:], key_v[:, 128:]
+    frame, key_frame = [], []
     for x in range(3):
-        shifted = opt[x] - column(anchor, x)
-        turned = sum(column(rot[x], y) * cotan[y] for y in range(3))
-        parts.append(
-            [total(dqg[x] * local[y]) + total(shifted * cotan[y]) for y in range(3)]
-            + [total(dqg[x]) - total(turned)]
-        )
-    put_frame(qfg_out, parts)
-
-    rot, anchor = frames(c * cols + r * share, share)
-    local_sel = pick(share, cols, r * share)
-    summed = kd_ref[...]
-    kg_out[...] = summed[:, 0:192]
-    dkg = [summed[:, 192 + 48 * x : 240 + 48 * x] for x in range(3)]
-    summed = kv_ref[...]
-    vg_out[...] = summed[:, 0:192]
-    dvg = [summed[:, 192 + 96 * x : 288 + 96 * x] for x in range(3)]
-    klocal = [take(local_sel, kp_ref[y]) for y in range(3)]
-    vlocal = [take(local_sel, vp_ref[y]) for y in range(3)]
-    for y in range(3):
-        kpg_out[y] = sum(column(rot[x], y) * dkg[x] for x in range(3))
-        vpg_out[y] = sum(column(rot[x], y) * dvg[x] for x in range(3))
-    parts = []
-    for x in range(3):
-        parts.append(
-            [total(dkg[x] * klocal[y]) + total(dvg[x] * vlocal[y]) for y in range(3)]
-            + [total(dkg[x]) + total(dvg[x])]
-        )
-    put_frame(kfg_out, parts)
-
-    bw_out[...] = small_ref[0:H, :]
+        both = lanes(512, x, (192, 48), (336, 96))
+        mask_d, mask_v = lanes(256, x, (192, 48)), lanes(384, x, (192, 96))
+        for y in range(4):
+            if y < 3:
+                one = segment_sum(query * handed(SEL_Q + 4 * y, 4), both)
+                two = segment_sum(key_d * handed(SEL_D + 2 * y, 2), mask_d)
+                three_ = segment_sum(key_v * handed(SEL_V + 3 * y, 3), mask_v)
+            else:
+                one = segment_sum(query, lanes(512, x, (192, 48)))
+                two, three_ = segment_sum(key_d, mask_d), segment_sum(key_v, mask_v)
+            frame.append(jnp.sum(one, axis=1, keepdims=True))
+            key_frame.append(jnp.sum(two + three_, axis=1, keepdims=True))
+    lines = frame_lines(frame, share)
+    put(
+        qfg_out,
+        [
+            line + sel_ref[SEL_C + n // share, n % share : n % share + 1, 0:share]
+            for n, line in enumerate(lines)
+        ],
+    )
+    put(kfg_out, frame_lines(key_frame, share))
+    for out, at, parts in turned:
+        width = parts[0].shape[1]
+        for y in range(3):
+            out[y] = sum(sel_ref[at + 3 * x + y, :, 0:width] * parts[x] for x in range(3))
+
+    for h in range(H):
+        bw_out[h : h + 1, :] = small_ref[8 * (h % 2) + h // 2 : 8 * (h % 2) + h // 2 + 1, :]
     raw = hw_ref[...]
-    hw_out[...] = small_ref[12:13, 0:H] * (-0.5 * LOGIT * POINT) / (1.0 + jnp.exp(-raw))
+    hw_out[...] = small_ref[6:7, 0:H] * (-0.5 * LOGIT * POINT) / (1.0 + jnp.exp(-raw))
 
 
 def per_device(
@@ -790,6 +859,7 @@
         jax.ShapeDtypeStruct((share, KV), F32),
         jax.ShapeDtypeStruct((qshare, QF), F32),
         jax.ShapeDtypeStruct((16, CZ), F32),
+        jax.ShapeDtypeStruct((SEL_C + 2, share, 128), F32),
     )
 
     def staged(width):
@@ -807,26 +877,33 @@
         return tuple(dma((n,)) for n in counts for _ in range(2))
 
     levels = (m1 * n0, m0 * n2, n1)
-    turned, kd_sum, kv_sum, query_sum, small_sum = pl.pallas_call(
+    turned, kd_sum, kv_sum, query_sum, small_sum, own_parts = pl.pallas_call(
         functools.partial(tile_kernel, sizes),
         name="tile",
         out_shape=sums,
         in_specs=[hbm] * (1 + len(operands)),
-        out_specs=(hbm,) * 5,
+        out_specs=(hbm,) * 6,
         scratch_shapes=[
             *[like(a) for a in operands],
             like(pair_rep),
             *[like(a) for a in sums],
-            buf(cols // 128, rows * 32, 128),
-            buf(H * rows, cols),
-            buf(H * rows, cols),
-            buf(H * rows, cols),
+            buf(128, 128),
+            buf(KD, 128),
+            buf(KV, 128),
+            buf(32, rows, cols),
+            buf(rows, CZ, cols, dtype=BF),
+            buf(rows, 32, CZ),
+            buf(rows, 32, cols, dtype=BF),
+            buf(16, rows, cols),
+            buf(16, rows, cols),
+            buf(H, rows, cols),
             buf(H * 32, rows),
             buf(H * 32, cols),
             buf(H * 48, rows),
             buf(H * 48, cols),
             buf(H * rows, 128),
             buf(8, 128),
+            buf(16, 128),
             buf(16, 128),
             buf(cols_n - 1, 16, 128),
             buf(H * 32, 3 * rows, dtype=BF),
@@ -862,13 +939,8 @@
         kv_sum,
         query_sum,
         small_sum,
+        own_parts,
         head_row,
-        query_points,
-        key_points,
-        value_points,
-        rotations,
-        translations,
-        grad_points_t,
     )
     results = (
         jax.ShapeDtypeStruct((qshare, 192), F32),
@@ -883,7 +955,7 @@
         jax.ShapeDtypeStruct((1, H), F32),
     )
     pair_grad, qg, qpg, qfg, kg, vg, kpg, vpg, kfg, bw, hw = pl.pallas_call(
-        functools.partial(finish_kernel, sizes),
+        finish_kernel,
         name="finish",
         out_shape=(jax.ShapeDtypeStruct(pair_rep.shape, BF), *results),
         in_specs=[hbm] * len(operands),
@@ -893,7 +965,7 @@
             *[like(a) for a in results],
             like(pair_rep),
             dma((len(operands),)),
-            dma((4,)),
+            dma((8,)),
             dma((len(results),)),
         ],
         compiler_params=pltpu.CompilerParams(**params),

time: 40.6 us -> 39 us (0.961)
  Pallas kernels: 39.2 us -> 37.5 us
    pallas_call x1, Pallas kernels: 34.5 us -> 33.5 us  [per_device(): pl.pallas_call(functools.partial(tile_kernel, sizes), name='tile', out_sh...]
    pallas_call x1, Pallas kernels: 4.7 us -> 3.97 us  [per_device(): pl.pallas_call(finish_kernel, name='finish', out_shape=(jax.ShapeDtypeStr...]
where the time goes in v3:
time: 39 us; the launch traced here: 38.8 us
  Pallas kernels  37.5 us (96%)
  between operations  1.3 us (3%)
    pallas_call x1, Pallas kernels, per_device(): pl.pallas_call(functools.partial(tile_kernel, sizes), name='tile', out_sh...  33.5 us
    pallas_call x1, Pallas kernels, per_device(): pl.pallas_call(finish_kernel, name='finish', out_shape=(jax.ShapeDtypeStr...  3.97 us

profile of v3, /device:TPU:1, one launch (start us, length us, event | category | flops | bytes accessed | tf_op | source)
XLA Modules:
  0.0 38.8 jit_solution(16725403024323984265)
XLA Ops:
  1.3 33.5 %tile.1 = (bf16[16,256,128]{2,1,0:T(8,128)(2,1)}, f32[8,384]{1,0:T(8,128)}, f32[8,512]{1,0:T(8,128)}, f32[8,640]{1,0:T(8,128)}, f32[16,128]{1,0:T(8,128)}, /*index=5*/f32[47,8,128]{2,1,0:T(8,128)}) custom-call(bf16[64,256,128]{2,1,0:T(8,128)(2,1)} %pair_hbm.1, bf16[12,128]{1,0:T(8,128)(2,1)} %bitcast.19, f32[1,12]{1,0:T(1,128)} %bitcast.21, ...), custom_call_target="tpu_custom_call" | custom-call | tf_op jit(solution)/shard_map/tile/pallas_call | solution.py:880
  34.8 4.0 %finish.1 = (bf16[64,256,128]{2,1,0:T(8,128)(2,1)}, f32[8,192]{1,0:T(8,128)}, f32[3,8,48]{2,1,0:T(8,128)}, f32[3,4,8]{2,1,0:T(4,128)}, f32[8,192]{1,0:T(8,128)},...) custom-call(bf16[16,256,128]{2,1,0:T(8,128)(2,1)} %get-tuple-element, ...), custom_call_target="tpu_custom_call" | custom-call | tf_op jit(solution)/shard_map/finish/pallas_call | solution.py:957

commit v4 on v3

--- a/solution.py
+++ b/solution.py
@@ -180,8 +180,8 @@
         return {"col_0": p // m1, "col_1": lax.rem(p, m1)}
 
     groups = {
+        "x": (m0 * n2, j0 * n2 + i2, lambda p: {"col_0": p // n2, "row_2": lax.rem(p, n2)}),
         "z": (m1 * n0, j1 * n0 + i0, lambda p: {"col_1": p // n0, "row_0": lax.rem(p, n0)}),
-        "x": (m0 * n2, j0 * n2 + i2, lambda p: {"col_0": p // n2, "row_2": lax.rem(p, n2)}),
         "y": (n1, i1, lambda p: {"row_1": p}),
     }
 
@@ -213,7 +213,7 @@
         pltpu.make_async_copy(src, dst, in_sem.at[n])
         for n, (src, dst) in enumerate(zip(inputs, copies_in))
     ]
-    for load in smalls + loads[:2]:
+    for load in smalls:
         load.start()
 
     barrier = pltpu.get_barrier_semaphore()
@@ -228,7 +228,7 @@
             )
             expected += 1
 
-    for load in loads[2:]:
+    for load in loads:
         load.start()
     for load in smalls:
         load.wait()
@@ -338,19 +338,19 @@
             lane == 0, peak + jnp.log(total), jnp.where(lane == 1, upper / total, peak)
         )
     blocks = H * rows // 128
-    stat_own[...] = jnp.zeros_like(stat_own)
     own_peak[...] = jnp.zeros_like(own_peak)
     own_dist[...] = jnp.zeros_like(own_dist)
     for b in range(blocks):
         turned = vec[128 * b : 128 * b + 128, :].T
         stat_own[b : b + 1, :] = turned[0:1]
-        stat_own[8 + b : 9 + b, :] = turned[1:2]
+        stat_own[blocks + b : blocks + b + 1, :] = turned[1:2]
         own_peak[b : b + 1, :] = turned[2:3]
 
     pl.semaphore_wait(barrier, expected)
 
     stat_copies = [
-        send(stat_own, stat_in.at[d - 1], stat_sems, d - 1, col_peer(d)) for d in range(1, cols_n)
+        send(stat_own, stat_in.at[d - 1], stat_sems, d - 1, col_peer(d))
+        for d in sorted(range(1, cols_n), key=lambda d: d % m1 == 0)
     ]
 
     for a in (6, 14, 22, 30):
@@ -388,13 +388,20 @@
     for copy in stat_copies:
         copy.wait()
 
-    stats = [stat_own[...]] + [stat_in[d] for d in range(cols_n - 1)]
-    peak = functools.reduce(jnp.maximum, [s[0:8] for s in stats])
-    weights = [jnp.exp(s[0:8] - peak) for s in stats]
+    def padded(ref, part):
+        rows_here = ref[part * blocks : part * blocks + blocks, :]
+        return jnp.concatenate([rows_here, jnp.zeros((8 - blocks, 128), F32)], axis=0)
+
+    stats = [
+        (padded(ref, 0), padded(ref, 1))
+        for ref in [stat_own] + [stat_in.at[d] for d in range(cols_n - 1)]
+    ]
+    peak = functools.reduce(jnp.maximum, [s[0] for s in stats])
+    weights = [jnp.exp(s[0] - peak) for s in stats]
     total = functools.reduce(jnp.add, weights)
-    delta = functools.reduce(jnp.add, [w * s[8:16] for w, s in zip(weights, stats)]) / total
+    delta = functools.reduce(jnp.add, [w * s[1] for w, s in zip(weights, stats)]) / total
     scale = jnp.exp(own_peak[...] - peak) / total
-    shift = delta - stats[0][8:16]
+    shift = delta - stats[0][1]
     scale_t, delta_t = scale.T, delta.T
 
     class Small:
@@ -442,7 +449,7 @@
     spread = jnp.where(lane8 == 2 * row8, even, jnp.where(lane8 == 2 * row8 + 1, odd, 0.0))
     head_sum = jnp.sum(spread, axis=0, keepdims=True)
     small = Small(jnp.where(iota((16, 1), 0) == 6, head_sum, LOGIT * acc))
-    small.send("z")
+    small.send("x")
 
     kind = iota((32, 1), 0)
     is_vec = kind < 16
@@ -459,13 +466,13 @@
             for a in range(self.feat.shape[0] // 128):
                 for b in range(cols // 128):
                     block = self.feat[128 * a : 128 * a + 128, 128 * b : 128 * b + 128].T
-                    self.kt[b * per : (b + 1) * per, :, :, 128 * a : 128 * a + 128] = block.reshape(
-                        per, n2, share, 128
-                    )
+                    block = block.reshape(per, n2, share, 128)
+                    for n in range(n2):
+                        self.kt[n, b * per : (b + 1) * per, :, 128 * a : 128 * a + 128] = block[:, n]
 
         def send1(self):
             other = lax.rem(i2 + 1, n2)
-            self.copies = [send(self.kt.at[:, other], self.k1, self.sems[0], 0, {"row_2": other})]
+            self.copies = [send(self.kt.at[other], self.k1, self.sems[0], 0, {"row_2": other})]
 
         def wait(self):
             for copy in self.copies:
@@ -473,17 +480,19 @@
 
         def send2(self):
             self.wait()
-            self.p1[...] = (self.kt[:, i2] + self.k1[...]).reshape(self.p1.shape)
+            for y in range(n1):
+                for z in range(n0):
+                    self.p1[y, z] = self.kt[i2, z * n1 + y] + self.k1[z * n1 + y]
             self.copies = []
             for d in range(1, n1):
                 to = lax.rem(i1 + d, n1)
                 self.copies.append(
-                    send(self.p1.at[:, to], self.k2.at[d - 1], self.sems[1], d - 1, {"row_1": to})
+                    send(self.p1.at[to], self.k2.at[d - 1], self.sems[1], d - 1, {"row_1": to})
                 )
 
         def send3(self):
             self.wait()
-            self.p2[...] = self.p1[:, i1] + functools.reduce(
+            self.p2[...] = self.p1[i1] + functools.reduce(
                 jnp.add, [self.k2[d] for d in range(n1 - 1)]
             )
             self.copies = []
@@ -532,8 +541,6 @@
     side_v.turn()
     side_v.send1()
 
-    side_d.send2()
-
     for h in range(H):
         at = (slice(h // 2, h // 2 + 1), slice(rows * (h % 2), rows * (h % 2) + rows))
         two = 2.0 * coef[:, h : h + 1]
@@ -560,7 +567,11 @@
             send(qt.at[pl.ds(to * m1, m1)], qx.at[d - 1], qx_sems, d - 1, {"col_0": to})
         )
 
+    side_d.send2()
+
     side_v.send2()
+    small.add()
+    small.send("z")
 
     for ib in range(rows // 8):
         some = slice(8 * ib, 8 * ib + 8)
@@ -627,9 +638,6 @@
     sel_copy = pltpu.make_async_copy(sel_out, sel_hbm, out_sem.at[5])
     sel_copy.start()
 
-    small.add()
-    small.send("x")
-    side_d.send3()
     for copy in qx_copies:
         copy.wait()
     qy[...] = qt[pl.ds(j0 * m1, m1)] + functools.reduce(jnp.add, [qx[d] for d in range(m0 - 1)])
@@ -637,6 +645,7 @@
     for d in range(1, m1):
         to = lax.rem(j1 + d, m1)
         qz_copies.append(send(qy.at[to], qz.at[d - 1], qz_sems, d - 1, {"col_1": to}))
+    side_d.send3()
     side_v.send3()
     small.add()
     small.send("y")
@@ -668,18 +677,11 @@
         pltpu.make_async_copy(src, dst, in_sem.at[n])
         for n, (src, dst) in enumerate(zip(inputs, copies_in))
     ]
-    for load in loads[3:] + loads[:3]:
+    for load in loads:
         load.start()
-    for load in loads[3:]:
-        load.wait()
-    finish_body(*copies_in[3:], *results)
-    stores = []
-    for n, (src, dst) in enumerate(zip(results, outs[1:])):
-        store = pltpu.make_async_copy(src, dst, out_sem.at[n])
-        store.start()
-        stores.append(store)
     for load in loads[:3]:
         load.wait()
+    stores = []
 
     rows = pg_v.shape[0]
     zero4 = jnp.zeros((4, CZ), F32)
@@ -712,6 +714,13 @@
             store.start()
             stores.append(store)
 
+    for load in loads[3:]:
+        load.wait()
+    finish_body(*copies_in[3:], *results)
+    for n, (src, dst) in enumerate(zip(results, outs[1:])):
+        store = pltpu.make_async_copy(src, dst, out_sem.at[n])
+        store.start()
+        stores.append(store)
     for store in stores:
         store.wait()
 
@@ -865,9 +874,9 @@
     def staged(width):
         return (
             buf(width, cols),
-            buf(n0 * n1, n2, share, width),
+            buf(n2, n0 * n1, share, width),
             buf(n0 * n1, share, width),
-            buf(n0, n1, share, width),
+            buf(n1, n0, share, width),
             buf(n1 - 1, n0, share, width),
             buf(n0, share, width),
             buf(n0 - 1, share, width),
@@ -876,7 +885,7 @@
     def pairs(*counts):
         return tuple(dma((n,)) for n in counts for _ in range(2))
 
-    levels = (m1 * n0, m0 * n2, n1)
+    levels = (m0 * n2, m1 * n0, n1)
     turned, kd_sum, kv_sum, query_sum, small_sum, own_parts = pl.pallas_call(
         functools.partial(tile_kernel, sizes),
         name="tile",
@@ -904,8 +913,8 @@
             buf(H * rows, 128),
             buf(8, 128),
             buf(16, 128),
-            buf(16, 128),
-            buf(cols_n - 1, 16, 128),
+            buf(2 * H * rows // 128, 128),
+            buf(cols_n - 1, 2 * H * rows // 128, 128),
             buf(H * 32, 3 * rows, dtype=BF),
             buf(H * 48, 3 * rows, dtype=BF),
             buf(H * 32, rows),
@@ -920,7 +929,7 @@
             staged(KV),
             tuple(b for n in levels for b in (buf(16, CZ), buf(n - 1, 16, CZ))),
             dma((len(operands),)),
-            dma((4,)),
+            dma((2,)),
             dma((len(sums),)),
             pairs(cols_n - 1),
             pairs(m0 - 1),

time: 39 us -> 38.2 us (0.979)
  Pallas kernels: 37.5 us -> 36.8 us
    pallas_call x1, Pallas kernels: 33.5 us -> 32.9 us  [per_device(): pl.pallas_call(functools.partial(tile_kernel, sizes), name='tile', out_sh...]
where the time goes in v4:
time: 38.2 us; the launch traced here: 38.1 us
  Pallas kernels  36.8 us (96%)
  between operations  1.3 us (3%)
    pallas_call x1, Pallas kernels, per_device(): pl.pallas_call(functools.partial(tile_kernel, sizes), name='tile', out_sh...  32.9 us
    pallas_call x1, Pallas kernels, per_device(): pl.pallas_call(finish_kernel, name='finish', out_shape=(jax.ShapeDtypeStr...  3.81 us

profile of v4, /device:TPU:1, one launch (start us, length us, event | category | flops | bytes accessed | tf_op | source)
XLA Modules:
  0.0 38.1 jit_solution(3944118091475013906)
XLA Ops:
  1.3 32.9 %tile.1 = (bf16[16,256,128]{2,1,0:T(8,128)(2,1)}, f32[8,384]{1,0:T(8,128)}, f32[8,512]{1,0:T(8,128)}, f32[8,640]{1,0:T(8,128)}, f32[16,128]{1,0:T(8,128)}, /*index=5*/f32[47,8,128]{2,1,0:T(8,128)}) custom-call(bf16[64,256,128]{2,1,0:T(8,128)(2,1)} %pair_hbm.1, bf16[12,128]{1,0:T(8,128)(2,1)} %bitcast.19, f32[1,12]{1,0:T(1,128)} %bitcast.21, ...), custom_call_target="tpu_custom_call" | custom-call | tf_op jit(solution)/shard_map/tile/pallas_call | solution.py:889
  34.2 3.8 %finish.1 = (bf16[64,256,128]{2,1,0:T(8,128)(2,1)}, f32[8,192]{1,0:T(8,128)}, f32[3,8,48]{2,1,0:T(8,128)}, f32[3,4,8]{2,1,0:T(4,128)}, f32[8,192]{1,0:T(8,128)},...) custom-call(bf16[16,256,128]{2,1,0:T(8,128)(2,1)} %get-tuple-element, ...), custom_call_target="tpu_custom_call" | custom-call | tf_op jit(solution)/shard_map/finish/pallas_call | solution.py:966

commit v5 on v4

--- a/solution.py
+++ b/solution.py
@@ -349,14 +349,31 @@
     pl.semaphore_wait(barrier, expected)
 
     stat_copies = [
-        send(stat_own, stat_in.at[d - 1], stat_sems, d - 1, col_peer(d))
+        pltpu.make_async_remote_copy(
+            src_ref=stat_own,
+            dst_ref=stat_in.at[d - 1],
+            send_sem=stat_sems[0].at[d - 1],
+            recv_sem=stat_sems[1].at[d - 1],
+            device_id=col_peer(d),
+            device_id_type=MESH,
+        )
         for d in sorted(range(1, cols_n), key=lambda d: d % m1 == 0)
     ]
+
+    def send_stats(core):
+        @pl.when(i2 == core)
+        def _():
+            for copy in stat_copies:
+                copy.start()
+
+    send_stats(0)
 
     for a in (6, 14, 22, 30):
         s_ref[a : a + 2] = jnp.zeros((2, rows, cols), F32)
     for h in range(H):
         own = slice(h * rows, (h + 1) * rows)
+        if h == 4:
+            send_stats(1)
         e = e_ref[h]
         es = split(e)
         ep = e * (p_ref[h] - vec[own, 1:2])

time: 38.2 us -> 38.5 us (level)
  no operation moved by 1% of the time
where the time goes in v5:
time: 38.5 us; the launch traced here: 38.4 us
  Pallas kernels  37.1 us (96%)
  between operations  1.3 us (3%)
    pallas_call x1, Pallas kernels, per_device(): pl.pallas_call(functools.partial(tile_kernel, sizes), name='tile', out_sh...  33.3 us
    pallas_call x1, Pallas kernels, per_device(): pl.pallas_call(finish_kernel, name='finish', out_shape=(jax.ShapeDtypeStr...  3.81 us

profile of v5, /device:TPU:1, one launch (start us, length us, event | category | flops | bytes accessed | tf_op | source)
XLA Modules:
  0.0 38.4 jit_solution(8673314402423151171)
XLA Ops:
  1.3 33.3 %tile.1 = (bf16[16,256,128]{2,1,0:T(8,128)(2,1)}, f32[8,384]{1,0:T(8,128)}, f32[8,512]{1,0:T(8,128)}, f32[8,640]{1,0:T(8,128)}, f32[16,128]{1,0:T(8,128)}, /*index=5*/f32[47,8,128]{2,1,0:T(8,128)}) custom-call(bf16[64,256,128]{2,1,0:T(8,128)(2,1)} %pair_hbm.1, bf16[12,128]{1,0:T(8,128)(2,1)} %bitcast.19, f32[1,12]{1,0:T(1,128)} %bitcast.21, ...), custom_call_target="tpu_custom_call" | custom-call | tf_op jit(solution)/shard_map/tile/pallas_call | solution.py:906
  34.6 3.8 %finish.1 = (bf16[64,256,128]{2,1,0:T(8,128)(2,1)}, f32[8,192]{1,0:T(8,128)}, f32[3,8,48]{2,1,0:T(8,128)}, f32[3,4,8]{2,1,0:T(4,128)}, f32[8,192]{1,0:T(8,128)},...) custom-call(bf16[16,256,128]{2,1,0:T(8,128)(2,1)} %get-tuple-element, ...), custom_call_target="tpu_custom_call" | custom-call | tf_op jit(solution)/shard_map/finish/pallas_call | solution.py:983
